TPU v7x, 128 devices: a whole 4x4x4 slice. The times are simulated.
128 devices in a mesh: tp: 16 (over z, y), dp: 8 (over x, core).
Axes of the slice: x: 4, y: 4, z: 4, core: 2. Of those that a mesh axis runs over, the one named last changes fastest.
Arguments:
- x_in: bfloat16 [2, 8192, 3072], P(None, ('dp', 'tp'))
- w_gate: bfloat16 [3072, 8192], P('dp', 'tp')
- w_up: bfloat16 [3072, 8192], P('dp', 'tp')
- w_down: bfloat16 [8192, 3072], P('tp', 'dp')
- grad_y: bfloat16 [2, 8192, 3072], P(None, ('dp', 'tp'))
Outputs:
- output 1: bfloat16 [2, 8192, 3072], P(None, ('dp', 'tp'))
- output 2: bfloat16 [2, 8192, 3072], P(None, ('dp', 'tp'))
- output 3: float32 [3072, 8192], P('dp', 'tp')
- output 4: float32 [3072, 8192], P('dp', 'tp')
- output 5: float32 [8192, 3072], P('tp', 'dp')
All inputs are finite; a program needn't handle non-finite values.
Results may differ from a plain program's by a relative error of at most 0.00102.
Values are sent between devices in bfloat16 or wider.
A program may use at most 1 GiB of HBM per device.

v0:
```python
import jax
import jax.numpy as jnp
from jax import lax
from jax.sharding import PartitionSpec as P


def gate_grads(grad_h, gate_pre, up_pre, sig_gate, act_gate):
    grad_gate = grad_h * up_pre * sig_gate * (1.0 + gate_pre * (1.0 - sig_gate))
    grad_up = grad_h * act_gate
    return grad_gate.astype(jnp.bfloat16), grad_up.astype(jnp.bfloat16)


def solution(mesh):
    data_size = mesh.shape["dp"]
    model_size = mesh.shape["tp"]
    row_spec = P(None, ("dp", "tp"), None)
    in_specs = (row_spec, P("dp", "tp"), P("dp", "tp"), P("tp", "dp"), row_spec)
    out_specs = (row_spec, row_spec, P("dp", "tp"), P("dp", "tp"), P("tp", "dp"))

    def token_columns(rows_loc):
        spread = lax.all_to_all(rows_loc, "dp", split_axis=1, concat_axis=0, tiled=True)
        gathered = lax.all_gather(spread, "tp", axis=0)
        return gathered.reshape(model_size, data_size, -1, gathered.shape[-1])

    def reduce_data(part_sum):
        return lax.psum_scatter(part_sum, "dp", scatter_dimension=1, tiled=True)[:, 0]

    def to_rows(part_sum):
        reduced = lax.psum_scatter(part_sum, "tp", scatter_dimension=0, tiled=True)[0]
        return lax.all_to_all(reduced, "dp", split_axis=0, concat_axis=2, tiled=True)[0]

    def local_step(x_loc, w_gate_loc, w_up_loc, w_down_loc, dy_loc):
        y_list = []
        dx_list = []
        for micro_idx in range(x_loc.shape[0]):
            x_cols = token_columns(x_loc[micro_idx])
            gate_pre = reduce_data(jnp.einsum("tkrd,df->tkrf", x_cols, w_gate_loc, preferred_element_type=jnp.float32))
            up_pre = reduce_data(jnp.einsum("tkrd,df->tkrf", x_cols, w_up_loc, preferred_element_type=jnp.float32))
            sig_gate = jax.nn.sigmoid(gate_pre)
            act_gate = gate_pre * sig_gate
            hidden = (act_gate * up_pre).astype(jnp.bfloat16)
            hidden_all = lax.all_gather(hidden, "dp", axis=1)
            out_sum = to_rows(jnp.einsum("tkrf,fd->tkrd", hidden_all, w_down_loc, preferred_element_type=jnp.float32))
            y_list.append((x_loc[micro_idx].astype(jnp.float32) + out_sum).astype(jnp.bfloat16))
            dy_cols = token_columns(dy_loc[micro_idx])
            grad_h = reduce_data(jnp.einsum("tkrd,fd->tkrf", dy_cols, w_down_loc, preferred_element_type=jnp.float32))
            grad_gate, grad_up = gate_grads(grad_h, gate_pre, up_pre, sig_gate, act_gate)
            gate_all = lax.all_gather(grad_gate, "dp", axis=1)
            up_all = lax.all_gather(grad_up, "dp", axis=1)
            dx_part = jnp.einsum("tkrf,df->tkrd", gate_all, w_gate_loc, preferred_element_type=jnp.float32) + jnp.einsum("tkrf,df->tkrd", up_all, w_up_loc, preferred_element_type=jnp.float32)
            dx_list.append((dy_loc[micro_idx].astype(jnp.float32) + to_rows(dx_part)).astype(jnp.bfloat16))
            dw_gate = jnp.einsum("tkrd,tkrf->df", x_cols, gate_all, preferred_element_type=jnp.float32)
            dw_up = jnp.einsum("tkrd,tkrf->df", x_cols, up_all, preferred_element_type=jnp.float32)
            dw_down = jnp.einsum("tkrf,tkrd->fd", hidden_all, dy_cols, preferred_element_type=jnp.float32)
            if micro_idx == 0:
                gate_sum, up_sum, down_sum = dw_gate, dw_up, dw_down
            else:
                gate_sum = gate_sum + dw_gate
                up_sum = up_sum + dw_up
                down_sum = down_sum + dw_down
        return jnp.stack(y_list), jnp.stack(dx_list), gate_sum, up_sum, down_sum

    return jax.shard_map(local_step, mesh=mesh, in_specs=in_specs, out_specs=out_specs, check_vma=False)
```

profile of v0, /device:TPU:1, one launch (start us, length us, event | category | flops | bytes accessed | tf_op | source)
XLA Modules:
  0.0 1988.0 jit_solution(17389348878245126204)
XLA Ops:
  8.6 13.6 all_to_all.124
  22.4 11.9 all_to_all.125
  35.7 11.9 all_to_all.126
  59.7 24.2 %all-gather.15.cloned.1.call-done = bf16[16,512,384]{2,1,0:T(8,128)(2,1)} async-done(((bf16[1,512,384]{2,1,0:T(8,128)(2,1)}), bf16[16,512,384]{2,1,0:T(8,128)(2,1)}) %all-gather.15.cloned.1.call-update) | async-done | bytes 6291472 | tf_op jit(solution)/shard_map/all_gather | solution.py:22
  95.0 51.7 %all-gather.11.cloned.1.call-done = bf16[16,512,384]{2,1,0:T(8,128)(2,1)} async-done(((bf16[1,512,384]{2,1,0:T(8,128)(2,1)}), bf16[16,512,384]{2,1,0:T(8,128)(2,1)}) %all-gather.11.cloned.1.call-update) | async-done | bytes 6291472 | tf_op jit(solution)/shard_map/all_gather | solution.py:22
  173.9 35.4 %all-gather.25.cloned.1.call-done = bf16[16,512,384]{2,1,0:T(8,128)(2,1)} async-done(((bf16[1,512,384]{2,1,0:T(8,128)(2,1)}), bf16[16,512,384]{2,1,0:T(8,128)(2,1)}) %all-gather.25.cloned.1.call-update) | async-done | bytes 6291472 | tf_op jit(solution)/shard_map/all_gather | solution.py:22
  220.4 51.6 %all-gather.19.cloned.1.call-done = bf16[16,512,384]{2,1,0:T(8,128)(2,1)} async-done(((bf16[1,512,384]{2,1,0:T(8,128)(2,1)}), bf16[16,512,384]{2,1,0:T(8,128)(2,1)}) %all-gather.19.cloned.1.call-update) | async-done | bytes 6291472 | tf_op jit(solution)/shard_map/all_gather | solution.py:22
  284.6 968.7 %all-reduce.13.cloned.1.call-done = (f32[16,8,64,512]{3,2,1,0:T(8,128)}, f32[16,8,64,512]{3,2,1,0:T(8,128)}, f32[16,8,64,512]{3,2,1,0:T(8,128)}, f32[16,8,64,512...) async-done(((f32[16,8,64,512]{3,2,1,0:T(8,128)}, f32[16,8,64,512]{3,2,1,0:T(8,128)}, f32[16,8,64,512]{3,2,1,0:T(8,128)}, ...) | async-done | bytes 100663312
  1271.0 40.1 %all-gather.27.cloned.1.call-done = bf16[16,8,64,512]{3,2,1,0:T(8,128)(2,1)} async-done(((bf16[16,1,64,512]{3,2,1,0:T(8,128)(2,1)}), bf16[16,8,64,512]{3,2,1,0:T(8,128)(2,1)}) %all-gather.27.cloned.1.call-update) | async-done | bytes 8388624 | tf_op jit(solution)/shard_map/all_gather | solution.py:48
  1311.1 12.5 fusion.89
  1323.6 39.0 %all-gather.29.cloned.1.call-done = bf16[16,8,64,512]{3,2,1,0:T(8,128)(2,1)} async-done(((bf16[16,1,64,512]{3,2,1,0:T(8,128)(2,1)}), bf16[16,8,64,512]{3,2,1,0:T(8,128)(2,1)}) %all-gather.29.cloned.1.call-update) | async-done | bytes 8388624 | tf_op jit(solution)/shard_map/all_gather | solution.py:49
  1362.5 16.1 convolution_add_fusion
  1378.9 35.1 %all-gather.21.cloned.1.call-done = bf16[16,8,64,512]{3,2,1,0:T(8,128)(2,1)} async-done(((bf16[16,1,64,512]{3,2,1,0:T(8,128)(2,1)}), bf16[16,8,64,512]{3,2,1,0:T(8,128)(2,1)}) %all-gather.21.cloned.1.call-update) | async-done | bytes 8388624 | tf_op jit(solution)/shard_map/all_gather | solution.py:48
  1414.0 12.6 fusion.91
  1426.6 38.9 %all-gather.23.cloned.1.call-done = bf16[16,8,64,512]{3,2,1,0:T(8,128)(2,1)} async-done(((bf16[16,1,64,512]{3,2,1,0:T(8,128)(2,1)}), bf16[16,8,64,512]{3,2,1,0:T(8,128)(2,1)}) %all-gather.23.cloned.1.call-update) | async-done | bytes 8388624 | tf_op jit(solution)/shard_map/all_gather | solution.py:49
  1465.5 16.2 convolution_add_fusion.1
  1481.7 35.1 %all-gather.17.cloned.1.call-done = bf16[16,8,64,512]{3,2,1,0:T(8,128)(2,1)} async-done(((bf16[16,1,64,512]{3,2,1,0:T(8,128)(2,1)}), bf16[16,8,64,512]{3,2,1,0:T(8,128)(2,1)}) %all-gather.17.cloned.1.call-update) | async-done | bytes 8388624 | tf_op jit(solution)/shard_map/all_gather | solution.py:42
  1516.8 12.5 fusion.79
  1529.5 38.7 %all-gather.13.cloned.1.call-done = bf16[16,8,64,512]{3,2,1,0:T(8,128)(2,1)} async-done(((bf16[16,1,64,512]{3,2,1,0:T(8,128)(2,1)}), bf16[16,8,64,512]{3,2,1,0:T(8,128)(2,1)}) %all-gather.13.cloned.1.call-update) | async-done | bytes 8388624 | tf_op jit(solution)/shard_map/all_gather | solution.py:42
  1568.2 12.5 fusion.81
  1597.7 66.9 %reduce-scatter.37.cloned.1.call-done = f32[1,8,64,384]{3,2,1,0:T(8,128)} async-done(((f32[16,8,64,384]{3,2,1,0:T(8,128)}), f32[1,8,64,384]{3,2,1,0:T(8,128)}) %reduce-scatter.37.cloned.1.call-update) | async-done | bytes 786448
  1679.7 81.3 %reduce-scatter.35.cloned.1.call-done = f32[1,8,64,384]{3,2,1,0:T(8,128)} async-done(((f32[16,8,64,384]{3,2,1,0:T(8,128)}), f32[1,8,64,384]{3,2,1,0:T(8,128)}) %reduce-scatter.35.cloned.1.call-update) | async-done | bytes 786448
  1778.3 79.0 %reduce-scatter.33.cloned.1.call-done = f32[1,8,64,384]{3,2,1,0:T(8,128)} async-done(((f32[16,8,64,384]{3,2,1,0:T(8,128)}), f32[1,8,64,384]{3,2,1,0:T(8,128)}) %reduce-scatter.33.cloned.1.call-update) | async-done | bytes 786448
  1874.1 79.5 %reduce-scatter.31.cloned.1.call-done = f32[1,8,64,384]{3,2,1,0:T(8,128)} async-done(((f32[16,8,64,384]{3,2,1,0:T(8,128)}), f32[1,8,64,384]{3,2,1,0:T(8,128)}) %reduce-scatter.31.cloned.1.call-update) | async-done | bytes 786448
  (98 shorter events, 188.7 us)
Async XLA Ops:
  7.2 150.6 %copy-start = (bf16[384,512]{1,0:T(8,128)(2,1)S(1)}, bf16[384,512]{1,0:T(8,128)(2,1)}, u32[]{:S(2)}) copy-start(bf16[384,512]{1,0:T(8,128)(2,1)} %param.6) | copy-start | bytes 1179652
  7.2 76.7 %copy-start.3 = (bf16[384,512]{1,0:T(8,128)(2,1)S(1)}, bf16[384,512]{1,0:T(8,128)(2,1)}, u32[]{:S(2)}) copy-start(bf16[384,512]{1,0:T(8,128)(2,1)} %param.7) | copy-start | bytes 1179652
  7.2 76.7 %all-gather.15.cloned.1.call-start = ((), (), s32[]{:S(2)}) async-start(), calls=%async_computation.14 | async-start | bytes 6684672 | tf_op jit(solution)/shard_map/all_gather | solution.py:22
  22.3 124.4 %all-gather.11.cloned.1.call-start = ((), (), s32[]{:S(2)}) async-start(), calls=%async_computation.12 | async-start | bytes 6684672 | tf_op jit(solution)/shard_map/all_gather | solution.py:22
  34.4 175.0 %all-gather.25.cloned.1.call-start = ((), (), s32[]{:S(2)}) async-start(), calls=%async_computation.19 | async-start | bytes 6684672 | tf_op jit(solution)/shard_map/all_gather | solution.py:22
  47.6 224.4 %all-gather.19.cloned.1.call-start = ((), (), s32[]{:S(2)}) async-start(), calls=%async_computation.16 | async-start | bytes 6684672 | tf_op jit(solution)/shard_map/all_gather | solution.py:22
  59.7 1193.6 %all-reduce.13.cloned.1.call-start = ((), (), s32[]{:S(2)}) async-start(), calls=%async_computation.26 | async-start | bytes 201326592
  146.6 11.2 copy-start.2
  146.6 19.3 slice-start
  165.9 43.5 %copy-start.4 = (bf16[512,384]{1,0:T(8,128)(2,1)S(1)}, bf16[512,384]{1,0:T(8,128)(2,1)}, u32[]{:S(2)}) copy-start(bf16[512,384]{1,0:T(8,128)(2,1)} %param.8) | copy-start | bytes 1179652
  283.4 1027.7 %all-gather.27.cloned.1.call-start = ((), (), s32[]{:S(2)}) async-start(), calls=%async_computation.20 | async-start | bytes 9437184 | tf_op jit(solution)/shard_map/all_gather | solution.py:48
  1260.4 102.1 %all-gather.29.cloned.1.call-start = ((), (), s32[]{:S(2)}) async-start(), calls=%async_computation.21 | async-start | bytes 9437184 | tf_op jit(solution)/shard_map/all_gather | solution.py:49
  1261.2 152.8 %all-gather.21.cloned.1.call-start = ((), (), s32[]{:S(2)}) async-start(), calls=%async_computation.17 | async-start | bytes 9437184 | tf_op jit(solution)/shard_map/all_gather | solution.py:48
  1268.3 197.1 %all-gather.23.cloned.1.call-start = ((), (), s32[]{:S(2)}) async-start(), calls=%async_computation.18 | async-start | bytes 9437184 | tf_op jit(solution)/shard_map/all_gather | solution.py:49
  1269.1 247.7 %all-gather.17.cloned.1.call-start = ((), (), s32[]{:S(2)}) async-start(), calls=%async_computation.15 | async-start | bytes 9437184 | tf_op jit(solution)/shard_map/all_gather | solution.py:42
  1269.7 298.5 %all-gather.13.cloned.1.call-start = ((), (), s32[]{:S(2)}) async-start(), calls=%async_computation.13 | async-start | bytes 9437184 | tf_op jit(solution)/shard_map/all_gather | solution.py:42
  1270.4 394.2 %reduce-scatter.37.cloned.1.call-start = ((), (), s32[]{:S(2)}) async-start(), calls=%async_computation.25 | async-start | bytes 13369344
  1378.7 382.3 %reduce-scatter.35.cloned.1.call-start = ((), (), s32[]{:S(2)}) async-start(), calls=%async_computation.24 | async-start | bytes 13369344
  1481.6 375.6 %reduce-scatter.33.cloned.1.call-start = ((), (), s32[]{:S(2)}) async-start(), calls=%async_computation.23 | async-start | bytes 13369344
  1529.2 424.3 %reduce-scatter.31.cloned.1.call-start = ((), (), s32[]{:S(2)}) async-start(), calls=%async_computation.22 | async-start | bytes 13369344
  1664.7 96.4 %all-to-all-start.7 = ((f32[8,64,384]{2,1,0:T(8,128)}), f32[8,64,384]{2,1,0:T(8,128)S(1)}, u32[]{:S(2)}, u32[]{:S(2)}) async-start(f32[8,64,384]{2,1,0:T(8,128)} %bitcast.210), calls=%async_computation.7 | async-start | bytes 1572864 | tf_op jit(solution)/shard_map/all_to_all | solution.py:30
  1761.0 96.3 %all-to-all-start.5 = ((f32[8,64,384]{2,1,0:T(8,128)}), f32[8,64,384]{2,1,0:T(8,128)S(1)}, u32[]{:S(2)}, u32[]{:S(2)}) async-start(f32[8,64,384]{2,1,0:T(8,128)} %bitcast.212), calls=%async_computation.5 | async-start | bytes 1572864 | tf_op jit(solution)/shard_map/all_to_all | solution.py:30
  1857.3 96.3 %all-to-all-start.3 = ((f32[8,64,384]{2,1,0:T(8,128)}), f32[8,64,384]{2,1,0:T(8,128)S(1)}, u32[]{:S(2)}, u32[]{:S(2)}) async-start(f32[8,64,384]{2,1,0:T(8,128)} %bitcast.211), calls=%async_computation.3 | async-start | bytes 1572864 | tf_op jit(solution)/shard_map/all_to_all | solution.py:30
  1953.6 23.7 %all-to-all-start.1 = ((f32[8,64,384]{2,1,0:T(8,128)}), f32[8,64,384]{2,1,0:T(8,128)S(1)}, u32[]{:S(2)}, u32[]{:S(2)}) async-start(f32[8,64,384]{2,1,0:T(8,128)} %bitcast.209), calls=%async_computation.1 | async-start | bytes 1572864 | tf_op jit(solution)/shard_map/all_to_all | solution.py:30
  (6 other events, 41.0 us)
Sparse Core Ops, SparseCore 0:
  22.4 61.4 all-gather.14
  86.0 60.5 all-gather.10
  148.8 60.5 all-gather.24
  211.4 60.5 all-gather.18
  283.5 969.7 all-reduce.12
  1260.5 50.4 all-gather.26
  1312.8 49.7 all-gather.28
  1364.2 49.7 all-gather.20
  1415.7 49.7 all-gather.22
  1467.0 49.7 all-gather.16
  1518.5 49.7 all-gather.12
  1571.5 93.1 reduce-scatter.36
  1668.1 92.8 reduce-scatter.34
  1764.3 92.9 reduce-scatter.32
  1860.6 92.9 reduce-scatter.30
where the time goes:
time: 2000 us; the launch traced here: 1990 us
  waiting for transfers between devices  1670 us (84%)
  matrix products  201 us (10%)
  blocking collectives  49.3 us (2%)
  starting transfers between devices  27 us (1%)
    unnamed x20, waiting for transfers between devices  1280 us
    all_gather x4, waiting for transfers between devices, token_columns(): gathered = lax.all_gather(spread, 'tp', axis=0)  163 us
    all_gather x2, waiting for transfers between devices, local_step(): up_all = lax.all_gather(grad_up, 'dp', axis=1)  77.9 us
    all_gather x2, waiting for transfers between devices, local_step(): gate_all = lax.all_gather(grad_gate, 'dp', axis=1)  75.2 us
    all_gather x2, waiting for transfers between devices, local_step(): hidden_all = lax.all_gather(hidden, 'dp', axis=1)  73.8 us
    all_to_all x4, blocking collectives, token_columns(): lax.all_to_all(rows_loc, 'dp', split_axis=1, concat_axis=0, tiled=True)  49.3 us
  transfers between devices with their start and end apart: 19, of which 15 were waited for; matrix products, arithmetic and copies ran while one was open for 10% of the time, Pallas kernels for 0%

commit v1 on v0

v1 whole, which is shorter than its diff:
```python
import functools
import heapq

import jax
import jax.numpy as jnp
from jax import lax
from jax.experimental import pallas as pl
from jax.experimental.pallas import tpu as pltpu
from jax.sharding import PartitionSpec as P

MESH = pl.DeviceIdType.MESH
F32 = jnp.float32
BF16 = jnp.bfloat16
ICI_RATE = 44.0e3
CORE_RATE = 550.0e3
HBM_RATE = 2.5e6
MARGIN = 1.0
STEPS = (
    "Hoa", "H-a", "H-b", "R-", "H+a", "H+b", "R+", "Q-",
    "H2a", "H2b", "Hob", "W0a", "W0b", "Q+", "R2", "Q2",
    "W1a", "W1b", "Ro", "Qo", "W2a", "W2b", "W3a", "W3b",
)


def nbytes(ref):
    size = jnp.dtype(ref.dtype).itemsize
    for n in ref.shape:
        size *= n
    return size


class Place:
    def __init__(self):
        t = lax.axis_index("tp")
        d = lax.axis_index("dp")
        z, y, x, c = t // 4, t % 4, d // 2, d % 2
        self.z, self.y, self.x, self.c = z, y, x, c
        self.b = y % 2
        self.a = y // 2
        self.zp, self.zm, self.z2 = (z + 1) % 4, (z + 3) % 4, (z + 2) % 4
        self.xp, self.xm, self.x2 = (x + 1) % 4, (x + 3) % 4, (x + 2) % 4

        def at(z, y, x, c):
            return {"tp": z * 4 + y, "dp": x * 2 + c}

        self.dev = {
            "z+": at(self.zp, y, x, c),
            "z-": at(self.zm, y, x, c),
            "x+": at(z, y, self.xp, c),
            "x-": at(z, y, self.xm, c),
            "tok": at(z, y + 1 - 2 * self.b, x, c),
            "wgt": at(z, 3 - y, x, c),
            "core": at(z, y, x, 1 - c),
        }

    def barrier(self):
        sem = pltpu.get_barrier_semaphore()
        for dev in self.dev.values():
            pl.semaphore_signal(sem, inc=1, device_id=dev, device_id_type=MESH)
        pl.semaphore_wait(sem, len(self.dev))


class Handle:
    def __init__(self, time, wait, after=None):
        self.time, self._wait, self.after, self.done = time, wait, after, False

    def wait(self):
        if not self.done:
            self.done = True
            self._wait()
            if self.after is not None:
                self.after()


class Flag:
    def __init__(self, count=1):
        self.left = count

    def hit(self):
        self.left -= 1


class Pool:
    def __init__(self, refs):
        self.refs = refs
        self.back = [[] for _ in refs]
        self.free = [True] * len(refs)

    def when_ready(self, count):
        times = sorted(max((h.time for h in self.back[i]), default=0.0) for i in range(len(self.refs)) if self.free[i])
        return times[count - 1] if len(times) >= count else float("inf")

    def take(self, count):
        order = sorted(
            (max((h.time for h in self.back[i]), default=0.0), i) for i in range(len(self.refs)) if self.free[i]
        )
        got = [i for _, i in order[:count]]
        for i in got:
            for h in self.back[i]:
                h.wait()
            self.back[i] = []
            self.free[i] = False
        return got

    def give(self, i, handles=()):
        self.free[i] = True
        self.back[i] = list(handles)


class Net:
    def __init__(self, place, local_sems, send_sems, recv_sems):
        self.place, self.local_sems, self.send_sems, self.recv_sems = place, local_sems, send_sems, recv_sems
        self.used = 0
        self.local_used = 0
        self.local_free = []
        self.open = []
        self.heap = []
        self.jobs = []
        self.seq = 0
        self.now = 0.0
        self.free = {}
        self.log = []

    def send(self, link, src, dst, land=None):
        land = dst if land is None else land
        i = self.used
        self.used += 1
        dev = self.place.dev[link]

        def copy_of(a, b):
            return pltpu.make_async_remote_copy(
                src_ref=a, dst_ref=b, send_sem=self.send_sems.at[i], recv_sem=self.recv_sems.at[i],
                device_id=dev, device_id_type=MESH,
            )

        copy = copy_of(src, dst)
        copy.start()
        arrive = copy_of(land, land)
        rate = CORE_RATE if link == "core" else ICI_RATE
        end = max(self.now, self.free.get(link, 0.0)) + nbytes(land) / rate
        self.free[link] = end
        sent = Handle(end + 0.5, copy.wait_send)
        self.open.append(sent)
        return Handle(end + 2.0, arrive.wait_recv), sent

    def copy(self, src, dst):
        if self.local_free:
            i = self.local_free.pop(0)
        else:
            i = self.local_used
            self.local_used += 1
        copy = pltpu.make_async_copy(src, dst, self.local_sems.at[i])
        copy.start()
        end = max(self.now, self.free.get("hbm", 0.0)) + nbytes(src) / HBM_RATE
        self.free["hbm"] = end
        handle = Handle(end + 0.8, copy.wait, lambda: self.local_free.append(i))
        self.open.append(handle)
        return handle

    def when(self, handles, then):
        self.seq += 1
        heapq.heappush(self.heap, (max(h.time for h in handles), self.seq, handles, then))

    def job(self, flags, needs, then, cost, rank, line=None):
        self.seq += 1
        self.jobs.append((rank, self.seq, flags, needs, then, cost, line))
        self.jobs.sort(key=lambda j: j[:2])

    def run(self):
        while True:
            if self.heap and self.heap[0][0] + MARGIN <= self.now:
                self.event()
                continue
            chosen = None
            soonest = float("inf")
            held = set()
            for j in self.jobs:
                if j[6] is not None:
                    if j[6] in held:
                        continue
                    held.add(j[6])
                if any(f.left > 0 for f in j[2]):
                    continue
                ready = max((pool.when_ready(n) for pool, n in j[3]), default=0.0)
                if ready <= self.now:
                    chosen = j
                    break
                soonest = min(soonest, ready)
            if chosen is not None:
                self.jobs.remove(chosen)
                _, _, _, needs, then, cost, _ = chosen
                slots = [pool.take(n) for pool, n in needs]
                self.now += cost
                then(*slots)
                continue
            if self.heap and self.heap[0][0] <= soonest:
                self.event()
            elif soonest < float("inf"):
                self.now = max(self.now, soonest)
            else:
                break
        assert not self.jobs, "jobs left"
        for handle in self.open:
            handle.wait()

    def event(self):
        time, _, handles, then = heapq.heappop(self.heap)
        self.now = max(self.now, time)
        for h in handles:
            h.wait()
        then()

    def arrive(self, handle, flag):
        self.when([handle], flag.hit)


def nothing():
    pass


def gather_ring_first(net, own, slot, half, ring, pair, me, each):
    r, rp, rm, r2, p = me
    up, down = ring
    from_down, _ = net.send(up, own, slot(r, p), slot(rm, p))
    from_up, _ = net.send(down, own, slot(r, p), slot(rp, p))
    other, _ = net.send(pair, own, slot(r, p), slot(r, 1 - p))
    net.when([other], lambda: each("o", 1, r, 1 - p))

    def pass_on(name, q):
        got, _ = net.send(pair, slot(q, p), slot(q, p), slot(q, 1 - p))
        net.when([got], lambda: each(name, 1, q, 1 - p))

    far = []

    def got_near(name, q, h, link):
        def then():
            ref = half(slot(q, p), h)
            far.append(net.send(link, ref, ref, half(slot(r2, p), h))[0])
            pass_on(name, q)
            each(name, 0, q, p)
            if len(far) == 2:
                net.when(far, got_far)
        return then

    def got_far():
        pass_on("2", r2)
        each("2", 0, r2, p)

    net.when([from_down], got_near("-", rm, 0, up))
    net.when([from_up], got_near("+", rp, 1, down))


def gather_pair_first(net, own, slot, half, ring, pair, me, each, late=False):
    r, rp, rm, r2, p = me
    up, down = ring

    def around(src, q, k):
        from_down, _ = net.send(up, src, slot(r, q), slot(rm, q))
        from_up, _ = net.send(down, src, slot(r, q), slot(rp, q))
        far = []

        def got_near(name, s, h, link):
            def then():
                ref = half(slot(s, q), h)
                far.append(net.send(link, ref, ref, half(slot(r2, q), h))[0])
                each(name, k, s, q)
                if k == 0 and late:
                    go_other()
                if len(far) == 2:
                    net.when(far, lambda: each("2", k, r2, q))
            return then

        net.when([from_down], got_near("-", rm, 0, up))
        net.when([from_up], got_near("+", rp, 1, down))

    other, _ = net.send(pair, own, slot(r, p), slot(r, 1 - p))
    before = Flag(3 if late else 1)

    def go_other():
        before.hit()
        if before.left == 0:
            around(slot(r, 1 - p), 1 - p, 1)

    def got_other():
        each("o", 1, r, 1 - p)
        go_other()

    net.when([other], got_other)
    around(own, p, 0)


def sum_rows(dst, srcs):
    if len(dst.shape) > 2:
        for i in range(dst.shape[0]):
            sum_rows(dst.at[i], [s.at[i] for s in srcs])
        return
    step = 16

    @pl.loop(0, dst.shape[0] // step)
    def _(i):
        at = pl.ds(pl.multiple_of(i * step, step), step)
        total = dst[at, :]
        for s in srcs:
            total = total + s[at, :]
        dst[at, :] = total


def dot(a, b, ca, cb):
    return lax.dot_general(a, b, (((ca,), (cb,)), ((), ())), preferred_element_type=F32)


def layer_kernel(
    x_ref, dy_ref, wg_ref, wu_ref, wd_ref,
    r_own, r_lp, q_own, q_l2, gu_own, gu_lp, d_own, d_l2,
    x_all, dy_all, r_pt, q_pt, w_pt, r_l1, r_l2, q_lp, q_l1, w_lc, gu_l1, gu_l2, d_lp, d_l1,
    wg_all, wu_all, wd_all, h_all, da_all, db_all, xb, db, xs, ds, r_out, q_out, tw, tk, wk,
    local_sems, send_sems, recv_sems,
):
    here = Place()
    here.barrier()
    net = Net(here, local_sems, send_sems, recv_sems)
    z, zp, zm, z2, b = here.z, here.zp, here.zm, here.z2, here.b
    x, xp, xm, x2, a, c = here.x, here.xp, here.xm, here.x2, here.a, here.c
    micro, rows, width = x_ref.shape
    wr, wc = wg_ref.shape
    edge = width // 8
    n_blk = 2 * micro * rows
    zs = {"o": z, "+": zp, "-": zm, "2": z2}
    xs_of = {"o": x, "+": xp, "-": xm, "2": x2}

    def rows_at(start, size):
        return pl.ds(pl.multiple_of(start, size), size)

    weights_in = [Flag(24), Flag(24)]
    tokens_in = {k: Flag(0) for k in zs}

    def up_slot(ref, core):
        return lambda q, p: ref.at[rows_at((q * 2 + core) * wr, wr), rows_at(p * wc, wc)]

    def down_slot(core):
        return lambda q, p: wd_all.at[rows_at(p * wc, wc), rows_at((q * 2 + core) * wr, wr)]

    def up_half(ref, h):
        return ref.at[pl.ds(h * (wr // 2), wr // 2)]

    def down_half(ref, h):
        return ref.at[pl.ds(h * (wc // 2), wc // 2)]

    def tok_half(ref, h):
        return ref.at[h]

    in_z = (z, zp, zm, z2, b)
    in_x = (x, xp, xm, x2, a)

    def across(mine, theirs):
        def each(name, k, q, p):
            weights_in[k].hit()
            got, _ = net.send("core", mine(q, p), mine(q, p), theirs(q, p))
            net.arrive(got, weights_in[k])
        return each

    def count_tokens(name, k, q, p):
        tokens_in[name].hit()

    for fn, own, mine, theirs, half in (
        (gather_ring_first, wg_ref, up_slot(wg_all, c), up_slot(wg_all, 1 - c), up_half),
        (functools.partial(gather_pair_first, late=True), wu_ref, up_slot(wu_all, c), up_slot(wu_all, 1 - c), up_half),
        (functools.partial(gather_pair_first, late=True), wd_ref, down_slot(c), down_slot(1 - c), down_half),
    ):
        fn(net, own, mine, half, ("x+", "x-"), "wgt", in_x, across(mine, theirs))
        got, _ = net.send("core", own, mine(x, a), theirs(x, a))
        net.arrive(got, weights_in[0])
        net.arrive(net.copy(own, mine(x, a)), weights_in[0])
    for name, f in tokens_in.items():
        f.left += 5 if name == "o" else 6
    for fn, own, dst, cols in (
        (gather_pair_first, x_ref, x_all, pl.ds(width - edge, edge)),
        (gather_ring_first, x_ref, x_all, pl.ds(0, width - edge)),
        (gather_pair_first, dy_ref, dy_all, pl.ds(0, width)),
    ):
        slot = functools.partial(lambda q, p, dst, cols: dst.at[q, p, :, :, cols], dst=dst, cols=cols)
        fn(net, own.at[:, :, cols], slot, tok_half, ("z+", "z-"), "tok", in_z, count_tokens)
    net.arrive(net.copy(x_ref, x_all.at[z, b]), tokens_in["o"])
    net.arrive(net.copy(dy_ref, dy_all.at[z, b]), tokens_in["o"])

    tok_pool = Pool([(xb.at[i], db.at[i]) for i in range(xb.shape[0])])
    cut_pool = Pool([(xs.at[i], ds.at[i]) for i in range(xs.shape[0])])
    r_pool = Pool([r_out.at[i] for i in range(r_out.shape[0])])
    q_pool = Pool([q_out.at[i] for i in range(q_out.shape[0])])
    wout_pool = Pool([tw.at[i] for i in range(tw.shape[0])])
    tk_pool = Pool([tk.at[i] for i in range(tk.shape[0])])
    wk_pool = Pool([wk.at[i] for i in range(wk.shape[0])])

    hidden = {k: Flag(2) for k in zs}
    tile_h = min(256, wc)

    def hidden_of(name, turn, rank):
        cols_at = a * wc if turn == 0 else (1 - a) * wc
        loaded = Flag()
        held = []

        def load(slots):
            i = slots[0]
            held.append(i)
            one, two = tok_pool.refs[i]
            first = net.copy(x_all.at[zs[name]], one)
            second = net.copy(dy_all.at[zs[name]], two)
            net.when([first, second], loaded.hit)

        def multiply():
            i = held[0]
            one, two = tok_pool.refs[i]
            at = rows_at(zs[name] * n_blk, n_blk)

            @pl.loop(0, wc // tile_h)
            def _(j):
                cols = rows_at(cols_at + j * tile_h, tile_h)
                x_blk = one[...].reshape(n_blk, width)
                dy_blk = two[...].reshape(n_blk, width)
                pre = dot(x_blk, wg_all[:, cols], 1, 0)
                up = dot(x_blk, wu_all[:, cols], 1, 0)
                g = dot(dy_blk, wd_all[cols, :], 1, 1)
                s = jax.nn.sigmoid(pre)
                act = pre * s
                h_all[at, cols] = (act * up).astype(BF16)
                da_all[at, cols] = (g * up * s * (1.0 + pre * (1.0 - s))).astype(BF16)
                db_all[at, cols] = (g * act).astype(BF16)

            tok_pool.give(i)
            hidden[name].hit()

        net.job([tokens_in[name]], [(tok_pool, 1)], load, 0.1, rank * 0.01, "load")
        net.job([loaded, weights_in[turn]], [], multiply, 2.8, rank, "mxu")

    r_in = {k: Flag() for k in zs}
    q_in = {k: Flag() for k in zs}
    tile_y = width // 2
    tile_dx = 2 * edge

    def rows_of(name, rank_r, rank_q):
        at = rows_at(zs[name] * n_blk, n_blk)
        s = zs[name]
        half_way = Flag()
        held = []

        def put(ref, cols, val):
            ref[:, :, :, cols] = val.reshape(2, micro, rows, val.shape[-1])

        def dx_tile(cols):
            return dot(da_all[at, :], wg_all[cols, :], 1, 1) + dot(db_all[at, :], wu_all[cols, :], 1, 1)

        def first(slots_r, slots_q):
            i = slots_r[0]
            ref = r_pool.refs[i]
            held.append(slots_q[0])

            @pl.loop(0, width // tile_y)
            def _(j):
                cols = rows_at(j * tile_y, tile_y)
                put(ref, cols, dot(h_all[at, :], wd_all[:, cols], 1, 0))

            val = dx_tile(pl.ds(0, tile_dx))
            put(ref, pl.ds(width, edge), val[:, :edge])
            put(q_pool.refs[held[0]], pl.ds(0, edge), val[:, edge:])
            done = net.copy(ref, r_pt.at[s])
            r_pool.give(i, [done])
            net.when([done], r_in[name].hit)
            half_way.hit()

        def second():
            i = held[0]
            ref = q_pool.refs[i]

            @pl.loop(1, width // tile_dx)
            def _(j):
                cols = rows_at(j * tile_dx, tile_dx)
                put(ref, pl.ds(pl.multiple_of(j * tile_dx - edge, edge), tile_dx), dx_tile(cols))

            done = net.copy(ref, q_pt.at[s])
            q_pool.give(i, [done])
            net.when([done], q_in[name].hit)

        net.job([hidden[name]], [(r_pool, 1), (q_pool, 1)], first, 3.0, rank_r, "mxu")
        net.job([half_way], [], second, 3.0, rank_q, "mxu")

    ranks = {step: 10 + i for i, step in enumerate(STEPS)}
    for name in zs:
        hidden_of(name, 0, ranks["H" + name + "a"])
        hidden_of(name, 1, ranks["H" + name + "b"])
        rows_of(name, ranks["R" + name], ranks["Q" + name])
    order = ("2", "+", "-", "o")

    def add_up(flags, pool, srcs, view, then, rank=1):
        def begin(slots):
            refs = [view(pool.refs[i]) for i in slots]
            loads = [net.copy(src, ref) for src, ref in zip(srcs, refs)]

            def add():
                sum_rows(refs[0], refs[1:])
                net.now += 0.25 * len(refs) * nbytes(refs[0]) / 1.0e6
                for i in slots[1:]:
                    pool.give(i)
                then(refs[0], slots[0])

            net.when(loads, add)

        net.job(flags, [(pool, len(srcs))], begin, 0.1, rank)

    def put_back(pool, ref, i, pairs, then):
        copies = [net.copy(src, dst) for src, dst in pairs]
        pool.give(i, copies)
        net.when(copies, then)

    y_from = {k: Flag() for k in ("z+", "z-")}
    y_near = [Flag(2), Flag(2)]

    def send_y2():
        for k, link in enumerate(("z+", "z-")):
            got, _ = net.send(link, r_pt.at[z2, :, k], r_l1.at[k])
            net.arrive(got, y_from[link])

    net.job([r_in["2"]], [], send_y2, 0.1, 1)

    def y_next(k, link, name):
        s = zs[name]

        def send_half(h):
            got, _ = net.send(link, r_pt.at[s, :, h], r_l2.at[k, h])
            net.arrive(got, y_near[h])

        net.job([r_in[name]], [], lambda: send_half(1 - k), 0.1, 1)

        def summed(ref, i):
            put_back(tk_pool, ref, i, [(ref, r_pt.at[s, :, k])], lambda: send_half(k))

        add_up([r_in[name], y_from[link]], tk_pool, [r_pt.at[s, :, k], r_l1.at[k]], lambda r: r, summed)

    y_next(0, "z+", "+")
    y_next(1, "z-", "-")

    def y_last(h):
        def summed(ref, i):
            def go():
                got, _ = net.send("tok", r_pt.at[z, 1 - b, h], r_lp.at[h])
                net.when([got], nothing)
            put_back(tk_pool, ref, i, [(ref.at[1 - b], r_pt.at[z, 1 - b, h]), (ref.at[b], r_own.at[h])], go)

        add_up([r_in["o"], y_near[h]], tk_pool, [r_pt.at[z, :, h], r_l2.at[0, h], r_l2.at[1, h]], lambda r: r, summed)

    y_last(0)
    y_last(1)

    def q_view(ref):
        return ref.at[:, :, pl.ds(0, width - edge)]

    dx_pair = {k: Flag() for k in zs}
    dx_from = {k: Flag() for k in ("z+", "z-")}

    def pair_dx(k, name):
        def go():
            got, _ = net.send("tok", q_pt.at[zs[name], 1 - b], q_lp.at[k])
            net.arrive(got, dx_pair[name])
        net.job([q_in[name]], [], go, 0.1, 1)

    for k, name in enumerate(order):
        pair_dx(k, name)

    def dx_far(ref, i):
        def go():
            for k, link in enumerate(("z+", "z-")):
                got, _ = net.send(link, q_pt.at[z2, b, k], q_l1.at[k])
                net.arrive(got, dx_from[link])
        put_back(tk_pool, ref, i, [(ref, q_pt.at[z2, b])], go)

    add_up([q_in["2"], dx_pair["2"]], tk_pool, [q_pt.at[z2, b], q_lp.at[0]], q_view, dx_far)

    def dx_next(k, link, name):
        s = zs[name]

        def half(h, flags, more):
            def summed(ref, i):
                def go():
                    got, _ = net.send(link, q_pt.at[s, b, h], q_l2.at[k, h])
                    net.when([got], nothing)
                put_back(tk_pool, ref, i, [(ref, q_pt.at[s, b, h])], go)
            srcs = [q_pt.at[s, b, h], q_lp.at[1 + k, h]] + more
            add_up([q_in[name], dx_pair[name]] + flags, tk_pool, srcs, lambda r: q_view(r).at[0], summed)

        half(1 - k, [], [])
        half(k, [dx_from[link]], [q_l1.at[k]])

    dx_next(0, "z+", "+")
    dx_next(1, "z-", "-")

    def dx_last(ref, i):
        put_back(tk_pool, ref, i, [(ref, q_own)], nothing)

    add_up([q_in["o"], dx_pair["o"]], tk_pool, [q_pt.at[z, b], q_lp.at[3]], q_view, dx_last)

    tile_w = wc
    n_tok = 4 * n_blk
    w_in = {(m, k): Flag() for m in range(3) for k in range(4)}
    w_side = {(m, k): Flag() for m in range(3) for k in range(4)}
    all_hidden = list(hidden.values())

    def grads_of(k, name, core, turn):
        loaded = Flag()
        held = []
        cols = rows_at((xs_of[name] * 2 + core) * wr, wr)

        def load(slots):
            i = slots[0]
            held.append(i)
            one, two = cut_pool.refs[i]
            first = net.copy(x_all.at[:, :, :, :, cols], one)
            second = net.copy(dy_all.at[:, :, :, :, cols], two)
            net.when([first, second], loaded.hit)

        def multiply(slots):
            i = held[0]
            one, two = cut_pool.refs[i]
            outs = [wout_pool.refs[j] for j in slots]

            @pl.loop(0, 2 * wc // tile_w)
            def _(j):
                at = rows_at(j * tile_w, tile_w)
                x_cut = one[...].reshape(n_tok, wr)
                dy_cut = two[...].reshape(n_tok, wr)
                outs[0][:, at] = dot(x_cut, da_all[:, at], 0, 0)
                outs[1][:, at] = dot(x_cut, db_all[:, at], 0, 0)
                outs[2][:, at] = dot(dy_cut, h_all[:, at], 0, 0)

            cut_pool.give(i)
            for m, (j, ref) in enumerate(zip(slots, outs)):
                if turn == 0:
                    got, sent = net.send("core", ref, w_lc.at[m, k])
                    wout_pool.give(j, [sent])
                    net.arrive(got, w_side[m, k])
                else:
                    done = net.copy(ref, w_pt.at[m, k])
                    wout_pool.give(j, [done])
                    net.when([done], w_in[m, k].hit)

        rank = ranks["W%d%s" % (k, "ab"[turn])]
        net.job(list(tokens_in.values()), [(cut_pool, 1)], load, 0.1, 2 + 0.01 * rank, "cut")
        net.job([loaded] + all_hidden, [(wout_pool, 3)], multiply, 2.9, rank, "mxu")

    for k, name in enumerate(order):
        grads_of(k, name, 1 - c, 0)
        grads_of(k, name, c, 1)

    hr = wr // 2

    def part(ref, h):
        return ref.at[pl.ds(h * hr, hr)]

    def w_ring_first(m):
        have = {k: [w_in[m, k], w_side[m, k]] for k in range(4)}
        come = [Flag(), Flag()]
        near = [Flag(2), Flag(2)]

        def far(h, link):
            def summed(ref, i):
                def go():
                    got, _ = net.send(link, part(w_pt.at[m, 0], h), gu_l1.at[m, h])
                    net.arrive(got, come[h])
                put_back(wk_pool, ref, i, [(ref, part(w_pt.at[m, 0], h))], go)
            add_up(have[0], wk_pool, [part(w_pt.at[m, 0], h), part(w_lc.at[m, 0], h)], lambda r: r, summed)

        far(0, "x+")
        far(1, "x-")

        def on(k, link):
            def half(h, flags, more):
                def summed(ref, i):
                    def go():
                        got, _ = net.send(link, part(w_pt.at[m, 1 + k], h), gu_l2.at[m, k, h])
                        net.arrive(got, near[h])
                    put_back(wk_pool, ref, i, [(ref, part(w_pt.at[m, 1 + k], h))], go)
                srcs = [part(w_pt.at[m, 1 + k], h), part(w_lc.at[m, 1 + k], h)] + more
                add_up(have[1 + k] + flags, wk_pool, srcs, lambda r: r, summed)
            half(1 - k, [], [])
            half(k, [come[k]], [gu_l1.at[m, k]])

        on(0, "x+")
        on(1, "x-")

        def last(h):
            def summed(ref, i):
                mine = ref.at[:, rows_at(a * wc, wc)]
                other = ref.at[:, rows_at((1 - a) * wc, wc)]
                away = part(w_pt.at[m, 3], h).at[:, rows_at((1 - a) * wc, wc)]

                def go():
                    got, _ = net.send("wgt", away, part(gu_lp.at[m], h))
                    net.when([got], nothing)
                put_back(wk_pool, ref, i, [(other, away), (mine, part(gu_own.at[m], h))], go)
            srcs = [part(w_pt.at[m, 3], h), part(w_lc.at[m, 3], h), gu_l2.at[m, 0, h], gu_l2.at[m, 1, h]]
            add_up(have[3] + [near[h]], wk_pool, srcs, lambda r: r, summed)

        last(0)
        last(1)

    def w_pair_first(m):
        mine = rows_at(a * wc, wc)
        other = rows_at((1 - a) * wc, wc)
        have = {k: [w_in[m, k], w_side[m, k]] for k in range(4)}
        pair = {(k, h): Flag() for k in range(4) for h in range(2)}
        come = [Flag(), Flag()]

        def view(r):
            return r.at[:, pl.ds(0, wc)]

        def away(k, h):
            dst = part(w_pt.at[m, k], h).at[:, other]

            def summed(ref, i):
                def go():
                    got, _ = net.send("wgt", dst, part(d_lp.at[k], h))
                    net.arrive(got, pair[k, h])
                put_back(wk_pool, ref, i, [(ref, dst)], go)
            add_up(have[k], wk_pool, [dst, part(w_lc.at[m, k], h).at[:, other]], view, summed)

        def stay(k, h, flags, more, dst, then):
            srcs = [part(w_pt.at[m, k], h).at[:, mine], part(w_lc.at[m, k], h).at[:, mine], part(d_lp.at[k], h)] + more

            def summed(ref, i):
                put_back(wk_pool, ref, i, [(ref, dst)], then)
            add_up(have[k] + [pair[k, h]] + flags, wk_pool, srcs, view, summed)

        for k in range(4):
            for h in range(2):
                away(k, h)

        def far(h, link):
            dst = part(w_pt.at[m, 0], h).at[:, mine]

            def go():
                got, _ = net.send(link, dst, d_l1.at[h])
                net.arrive(got, come[h])
            stay(0, h, [], [], dst, go)

        far(0, "x+")
        far(1, "x-")

        def on(k, link, h):
            dst = part(w_pt.at[m, 1 + k], h).at[:, mine]

            def go():
                got, _ = net.send(link, dst, d_l2.at[k, h])
                net.when([got], nothing)
            same = h == k
            stay(1 + k, h, [come[k]] if same else [], [d_l1.at[k]] if same else [], dst, go)

        for k, link in enumerate(("x+", "x-")):
            on(k, link, 1 - k)
            on(k, link, k)
        for h in range(2):
            stay(3, h, [], [], part(d_own, h), nothing)

    w_ring_first(0)
    w_ring_first(1)
    w_pair_first(2)
    net.run()


def solution(mesh):
    row_spec = P(None, ("dp", "tp"), None)
    in_specs = (row_spec, P("dp", "tp"), P("dp", "tp"), P("tp", "dp"), row_spec)
    out_specs = (row_spec, row_spec, P("dp", "tp"), P("dp", "tp"), P("tp", "dp"))
    vmem = pl.BlockSpec(memory_space=pltpu.VMEM)
    hbm = pl.BlockSpec(memory_space=pl.ANY)
    dma = pltpu.SemaphoreType.DMA
    V = pltpu.VMEM
    S = jax.ShapeDtypeStruct

    def local_step(x_loc, wg, wu, wd, dy_loc):
        micro, rows, width = x_loc.shape
        wr, wc = wg.shape
        edge = width // 8
        tok = (micro, rows, width)
        tok_r = (micro, rows, width + edge)
        tok_q = (micro, rows, width - edge)
        n = 8 * micro * rows
        outs = [
            S(tok_r, F32), S(tok_r, F32), S(tok_q, F32), S((2,) + tok_q, F32),
            S((2, wr, wc), F32), S((2, wr, wc), F32), S((wr, wc), F32), S((2, 2, wr // 2, wc), F32),
        ]
        space = [
            S((4, 2) + tok, BF16), S((4, 2) + tok, BF16), S((4, 2) + tok_r, F32), S((4, 2) + tok_q, F32),
            S((3, 4, wr, 2 * wc), F32),
            S((2, 2) + tok_r[1:], F32), S((2, 2, 2) + tok_r[1:], F32),
            S((4,) + tok_q, F32), S((2,) + tok_q[1:], F32),
            S((3, 4, wr, 2 * wc), F32),
            S((2, 2, wr // 2, 2 * wc), F32), S((2, 2, 2, wr // 2, 2 * wc), F32),
            S((4, wr, wc), F32), S((2, wr // 2, wc), F32),
        ]
        res = pl.pallas_call(
            layer_kernel,
            name="layer",
            out_shape=tuple(outs + space),
            in_specs=[vmem] * 2 + [hbm] * 3,
            out_specs=[hbm] * (len(outs) + len(space)),
            scratch_shapes=[
                V((width, 2 * wc), BF16), V((width, 2 * wc), BF16), V((2 * wc, width), BF16),
                V((n, 2 * wc), BF16), V((n, 2 * wc), BF16), V((n, 2 * wc), BF16),
                V((2, 2) + tok, BF16), V((2, 2) + tok, BF16),
                V((2, 4, 2, micro, rows, wr), BF16), V((2, 4, 2, micro, rows, wr), BF16),
                V((1, 2) + tok_r, F32), V((2, 2) + tok_q, F32), V((6, wr, 2 * wc), F32),
                V((3, 2) + tok_r[1:], F32), V((6, wr // 2, 2 * wc), F32),
                dma((96,)), dma((144,)), dma((144,)),
            ],
            compiler_params=pltpu.CompilerParams(
                collective_id=0, has_side_effects=True, vmem_limit_bytes=67_000_000
            ),
        )(x_loc, dy_loc, wg, wu, wd)
        r_own, r_lp, q_own, q_l2, gu_own, gu_lp, d_own, d_l2 = res[: len(outs)]
        r = r_own + r_lp
        q = q_own + q_l2[0] + q_l2[1]
        y = (x_loc.astype(F32) + r[:, :, :width]).astype(BF16)
        dx = (dy_loc.astype(F32) + jnp.concatenate([r[:, :, width:], q], axis=2)).astype(BF16)
        d_sum = d_own + d_l2[0].reshape(wr, wc) + d_l2[1].reshape(wr, wc)
        return y, dx, gu_own[0] + gu_lp[0], gu_own[1] + gu_lp[1], d_sum.T

    return jax.shard_map(local_step, mesh=mesh, in_specs=in_specs, out_specs=out_specs, check_vma=False)
```

time: 2000 us -> 280 us (0.14)
  waiting for transfers between devices: 1670 us -> 0 us
  Pallas kernels: 0 us -> 266 us
  matrix products: 201 us -> 0 us
  blocking collectives: 49.3 us -> 0 us
  starting transfers between devices: 27 us -> 0 us
    unnamed x20 -> x0, waiting for transfers between devices: 1280 us -> none
    all_gather x10 -> x0, waiting for transfers between devices: 390 us -> none  [the longest x4 163 us: token_columns(): gathered = lax.all_gather(spread, 'tp', axis=0)]
    pallas_call x0 -> x1, Pallas kernels: none -> 266 us  [local_step(): pl.pallas_call(layer_kernel, name='layer', out_shape=tuple(outs + space),...]
    dot_general x18 -> x0, matrix products: 201 us -> none  [the longest x2 32.3 us: local_step(): jnp.einsum('tkrf,df->tkrd', up_all, w_up_loc, preferred_element_type=jnp....]
    all_to_all x4 -> x0, blocking collectives: 49.3 us -> none  [token_columns(): lax.all_to_all(rows_loc, 'dp', split_axis=1, concat_axis=0, tiled=True)]
    all_to_all x4 -> x0, starting transfers between devices: 25.5 us -> none  [to_rows(): lax.all_to_all(reduced, 'dp', split_axis=0, concat_axis=2, tiled=True)[0]]
  transfers between devices with their start and end apart: 19 -> 0, of which waited for: 15 -> 0; matrix products, arithmetic and copies ran while one was open for 10% -> 0% of each run, Pallas kernels for 0% -> 0%
where the time goes in v1:
time: 280 us; the launch traced here: 278 us
  Pallas kernels  266 us (95%)
  other arithmetic  5.8 us (2%)
  local copies, waits for them, and re-layouts  5.42 us (2%)
    pallas_call x1, Pallas kernels, local_step(): pl.pallas_call(layer_kernel, name='layer', out_shape=tuple(outs + space),...  266 us

profile of v1, /device:TPU:1, one launch (start us, length us, event | category | flops | bytes accessed | tf_op | source)
XLA Modules:
  0.0 278.0 jit_solution(8125381341392935955)
XLA Ops:
  0.6 266.1 %layer.1 = (f32[2,64,3456]{2,1,0:T(8,128)}, f32[2,64,3456]{2,1,0:T(8,128)}, f32[2,64,2688]{2,1,0:T(8,128)}, f32[2,2,64,2688]{3,2,1,0:T(8,128)}, f32[2,384,512]{2...) custom-call(bf16[2,64,3072]{2,1,0:T(8,128)(2,1)} %x_ref.1, ...), custom_call_target="tpu_custom_call" | custom-call | tf_op jit(solution)/shard_map/layer/pallas_call | solution.py:798
  266.7 0.0 copy-start.2
  266.8 0.0 copy-start.6
  266.8 2.3 add.33
  269.1 0.5 copy-done.2
  269.6 0.4 copy-done.6
  270.0 0.0 copy-start
  270.0 0.0 copy-start.1
  270.0 0.2 bitcast_add_fusion
  270.2 0.9 copy-done
  271.1 0.2 copy-done.1
  271.3 0.0 copy-start.4
  271.3 0.0 copy-start.5
  271.3 1.6 fusion
  272.9 0.0 copy-done.4
  272.9 0.9 copy-done.5
  273.8 0.0 copy-start.3
  273.8 1.5 add_bitcast_fusion
  275.3 0.2 copy-done.3
  275.5 0.0 copy-start.7
  275.5 0.1 fusion.2
  275.6 1.0 copy-done.7
  276.6 0.2 bitcast_add_fusion.2
  276.9 1.1 copy.10
  (1 shorter events, 0.0 us)
Async XLA Ops:
  266.7 2.8 %copy-start.2 = (f32[2,2,64,2688]{3,2,1,0:T(8,128)S(1)}, f32[2,2,64,2688]{3,2,1,0:T(8,128)}, u32[]{:S(2)}) copy-start(f32[2,2,64,2688]{3,2,1,0:T(8,128)} %get-tuple-element.16) | copy-start | bytes 8257540
  266.8 3.2 %copy-start.6 = (f32[2,64,2688]{2,1,0:T(8,128)S(1)}, f32[2,64,2688]{2,1,0:T(8,128)}, u32[]{:S(2)}) copy-start(f32[2,64,2688]{2,1,0:T(8,128)} %get-tuple-element.15) | copy-start | bytes 4128772
  270.0 1.1 copy-start
  270.0 1.4 copy-start.1
  271.3 1.6 copy-start.4
  271.3 2.4 copy-start.5
  273.8 1.7 copy-start.3
  275.5 1.1 copy-start.7

commit v2 on v1

v2 whole, which is shorter than its diff:
```python
import functools
import heapq

import jax
import jax.numpy as jnp
from jax import lax
from jax.experimental import pallas as pl
from jax.experimental.pallas import tpu as pltpu
from jax.sharding import PartitionSpec as P

MESH = pl.DeviceIdType.MESH
F32 = jnp.float32
BF16 = jnp.bfloat16
ICI_RATE = 45.0e3
CORE_RATE = 550.0e3
HBM_RATE = 2.5e6
MARGIN = 1.0
STEPS = (
    "Hoa", "H-a", "Hob", "H-b", "H+b", "R-", "H+a", "H2b", "H2a", "R2",
    "W0a", "W0b", "Q2", "Y0", "Y2", "R+", "W2a", "W2b", "W1a", "W3a",
    "W1b", "Ro", "Q-", "Y1", "Y3", "Q+", "Qo", "W3b",
)


def nbytes(ref):
    size = jnp.dtype(ref.dtype).itemsize
    for n in ref.shape:
        size *= n
    return size


class Place:
    def __init__(self):
        t = lax.axis_index("tp")
        d = lax.axis_index("dp")
        z, y, x, c = t // 4, t % 4, d // 2, d % 2
        self.z, self.y, self.x, self.c = z, y, x, c
        self.b = y % 2
        self.a = y // 2
        self.zp, self.zm, self.z2 = (z + 1) % 4, (z + 3) % 4, (z + 2) % 4
        self.xp, self.xm, self.x2 = (x + 1) % 4, (x + 3) % 4, (x + 2) % 4

        def at(z, y, x, c):
            return {"tp": z * 4 + y, "dp": x * 2 + c}

        self.dev = {
            "z+": at(self.zp, y, x, c),
            "z-": at(self.zm, y, x, c),
            "x+": at(z, y, self.xp, c),
            "x-": at(z, y, self.xm, c),
            "tok": at(z, y + 1 - 2 * self.b, x, c),
            "wgt": at(z, 3 - y, x, c),
            "core": at(z, y, x, 1 - c),
        }

    def barrier(self):
        sem = pltpu.get_barrier_semaphore()
        for dev in self.dev.values():
            pl.semaphore_signal(sem, inc=1, device_id=dev, device_id_type=MESH)
        pl.semaphore_wait(sem, len(self.dev))


class Handle:
    def __init__(self, time, wait, after=None):
        self.time, self._wait, self.after, self.done = time, wait, after, False

    def wait(self):
        if not self.done:
            self.done = True
            self._wait()
            if self.after is not None:
                self.after()


class Flag:
    def __init__(self, count=1):
        self.left = count

    def hit(self):
        self.left -= 1


class Pool:
    def __init__(self, refs):
        self.refs = refs
        self.back = [[] for _ in refs]
        self.free = [True] * len(refs)

    def when_ready(self, count):
        times = sorted(max((h.time for h in self.back[i]), default=0.0) for i in range(len(self.refs)) if self.free[i])
        return times[count - 1] if len(times) >= count else float("inf")

    def take(self, count):
        order = sorted(
            (max((h.time for h in self.back[i]), default=0.0), i) for i in range(len(self.refs)) if self.free[i]
        )
        got = [i for _, i in order[:count]]
        for i in got:
            for h in self.back[i]:
                h.wait()
            self.back[i] = []
            self.free[i] = False
        return got

    def give(self, i, handles=()):
        self.free[i] = True
        self.back[i] = list(handles)


class Net:
    def __init__(self, place, local_sems, send_sems, recv_sems):
        self.place, self.local_sems, self.send_sems, self.recv_sems = place, local_sems, send_sems, recv_sems
        self.used = 0
        self.local_used = 0
        self.local_free = []
        self.open = []
        self.heap = []
        self.jobs = []
        self.seq = 0
        self.now = 0.0
        self.free = {}
        self.log = []

    def send(self, link, src, dst, land=None):
        land = dst if land is None else land
        i = self.used
        self.used += 1
        dev = self.place.dev[link]

        def copy_of(a, b):
            return pltpu.make_async_remote_copy(
                src_ref=a, dst_ref=b, send_sem=self.send_sems.at[i], recv_sem=self.recv_sems.at[i],
                device_id=dev, device_id_type=MESH,
            )

        copy = copy_of(src, dst)
        copy.start()
        arrive = copy_of(land, land)
        rate = CORE_RATE if link == "core" else ICI_RATE
        end = max(self.now, self.free.get(link, 0.0)) + nbytes(land) / rate
        self.free[link] = end
        sent = Handle(end + 0.5, copy.wait_send)
        self.open.append(sent)
        return Handle(end + 2.0, arrive.wait_recv), sent

    def copy(self, src, dst):
        if self.local_free:
            i = self.local_free.pop(0)
        else:
            i = self.local_used
            self.local_used += 1
        copy = pltpu.make_async_copy(src, dst, self.local_sems.at[i])
        copy.start()
        end = max(self.now, self.free.get("hbm", 0.0)) + nbytes(src) / HBM_RATE
        self.free["hbm"] = end
        handle = Handle(end + 0.8, copy.wait, lambda: self.local_free.append(i))
        self.open.append(handle)
        return handle

    def when(self, handles, then):
        self.seq += 1
        heapq.heappush(self.heap, (max(h.time for h in handles), self.seq, handles, then))

    def job(self, flags, needs, then, cost, rank, line=None):
        self.seq += 1
        self.jobs.append((rank, self.seq, flags, needs, then, cost, line))
        self.jobs.sort(key=lambda j: j[:2])

    def run(self):
        while True:
            if self.heap and self.heap[0][0] + MARGIN <= self.now:
                self.event()
                continue
            chosen = None
            soonest = float("inf")
            held = set()
            for j in self.jobs:
                if j[6] is not None:
                    if j[6] in held:
                        continue
                    held.add(j[6])
                if any(f.left > 0 for f in j[2]):
                    continue
                ready = max((pool.when_ready(n) for pool, n in j[3]), default=0.0)
                if ready <= self.now:
                    chosen = j
                    break
                soonest = min(soonest, ready)
            if chosen is not None:
                self.jobs.remove(chosen)
                _, _, _, needs, then, cost, _ = chosen
                slots = [pool.take(n) for pool, n in needs]
                self.now += cost
                then(*slots)
                continue
            if self.heap and self.heap[0][0] <= soonest:
                self.event()
            elif soonest < float("inf"):
                self.now = max(self.now, soonest)
            else:
                break
        assert not self.jobs, "jobs left"
        for handle in self.open:
            handle.wait()

    def event(self):
        time, _, handles, then = heapq.heappop(self.heap)
        self.now = max(self.now, time)
        for h in handles:
            h.wait()
        then()

    def arrive(self, handle, flag):
        self.when([handle], flag.hit)


def nothing():
    pass


def gather_ring_first(net, own, slot, half, ring, pair, me, each):
    r, rp, rm, r2, p = me
    up, down = ring
    from_down, _ = net.send(up, own, slot(r, p), slot(rm, p))
    from_up, _ = net.send(down, own, slot(r, p), slot(rp, p))
    other, _ = net.send(pair, own, slot(r, p), slot(r, 1 - p))
    net.when([other], lambda: each("o", 1, r, 1 - p))

    def pass_on(name, q):
        got, _ = net.send(pair, slot(q, p), slot(q, p), slot(q, 1 - p))
        net.when([got], lambda: each(name, 1, q, 1 - p))

    far = []

    def got_near(name, q, h, link):
        def then():
            ref = half(slot(q, p), h)
            far.append(net.send(link, ref, ref, half(slot(r2, p), h))[0])
            pass_on(name, q)
            each(name, 0, q, p)
            if len(far) == 2:
                net.when(far, got_far)
        return then

    def got_far():
        pass_on("2", r2)
        each("2", 0, r2, p)

    net.when([from_down], got_near("-", rm, 0, up))
    net.when([from_up], got_near("+", rp, 1, down))


def gather_pair_first(net, own, slot, half, ring, pair, me, each, late=False):
    r, rp, rm, r2, p = me
    up, down = ring

    def around(src, q, k):
        from_down, _ = net.send(up, src, slot(r, q), slot(rm, q))
        from_up, _ = net.send(down, src, slot(r, q), slot(rp, q))
        far = []

        def got_near(name, s, h, link):
            def then():
                ref = half(slot(s, q), h)
                far.append(net.send(link, ref, ref, half(slot(r2, q), h))[0])
                each(name, k, s, q)
                if k == 0 and late:
                    go_other()
                if len(far) == 2:
                    net.when(far, lambda: each("2", k, r2, q))
            return then

        net.when([from_down], got_near("-", rm, 0, up))
        net.when([from_up], got_near("+", rp, 1, down))

    other, _ = net.send(pair, own, slot(r, p), slot(r, 1 - p))
    before = Flag(3 if late else 1)

    def go_other():
        before.hit()
        if before.left == 0:
            around(slot(r, 1 - p), 1 - p, 1)

    def got_other():
        each("o", 1, r, 1 - p)
        go_other()

    net.when([other], got_other)
    around(own, p, 0)


def sum_rows(dst, srcs):
    if len(dst.shape) > 2:
        for i in range(dst.shape[0]):
            sum_rows(dst.at[i], [s.at[i] for s in srcs])
        return
    step = 16

    @pl.loop(0, dst.shape[0] // step)
    def _(i):
        at = pl.ds(pl.multiple_of(i * step, step), step)
        total = dst[at, :]
        for s in srcs:
            total = total + s[at, :]
        dst[at, :] = total


def dot(a, b, ca, cb):
    return lax.dot_general(a, b, (((ca,), (cb,)), ((), ())), preferred_element_type=F32)


def nth(refs, i, n):
    size = refs.shape[0] // n
    return refs.at[pl.ds(i * size, size)]


ORDER = ("2", "+", "-", "o")


class Adder:
    def __init__(self, net, pool, view):
        self.net, self.pool, self.view = net, pool, view

    def add(self, flags, srcs, outs, then):
        net, pool = self.net, self.pool

        def begin(slots):
            refs = [self.view(pool.refs[i], srcs[0].shape) for i in slots]
            loads = [net.copy(src, ref) for src, ref in zip(srcs, refs)]

            def done():
                sum_rows(refs[0], refs[1:])
                net.now += 0.25 * len(refs) * nbytes(refs[0]) / 1.0e6
                for i in slots[1:]:
                    pool.give(i)
                copies = [net.copy(src, dst) for src, dst in outs(refs[0])]
                pool.give(slots[0], copies)
                net.when(copies, then)

            net.when(loads, done)

        net.job(flags, [(pool, len(srcs))], begin, 0.1, 1)


def ring_reduce(net, adder, ready, srcs, l1, l2, links, near):
    come = [Flag(), Flag()]

    def go(name, h, more, flags, link, dst, flag):
        terms = srcs(name, h) + more

        def send():
            got, _ = net.send(link, terms[0], dst)
            net.arrive(got, flag)

        if len(terms) == 1:
            net.job(ready(name, h) + flags, [], send, 0.1, 1)
        else:
            adder.add(ready(name, h) + flags, terms, lambda ref: [(ref, terms[0])], send)

    for h, link in enumerate(links):
        go("2", h, [], [], link, l1.at[h], come[h])
    for k, (link, name) in enumerate(zip(links, "+-")):
        go(name, 1 - k, [], [], link, l2.at[k, 1 - k], near[1 - k])
        go(name, k, [l1.at[k]], [come[k]], link, l2.at[k, k], near[k])


def layer_kernel(
    x_ref, dy_ref, wg_ref, wu_ref, wd_ref,
    y_own, y_l2, r_own, r_lp, q_own, q_l2, g_own, g_lp, u_own, u_lp, v_own, v_l2, d_own, d_l2,
    x_all, dy_all, wd_ext, y_pt, r_pt, q_pt, w_pt, y_l1, r_l1, r_l2, q_lp, q_l1, w_lc,
    g_l1, g_l2, u_l1, u_l2, v_lp, v_l1, d_lp, d_l1,
    wg_all, wu_all, wd_all, h_all, da_all, db_all, h_ext, xb, db, xs, ds, r_out, q_out, y_out, wx, tw, tk, wk,
    local_sems, send_sems, recv_sems,
):
    here = Place()
    here.barrier()
    net = Net(here, local_sems, send_sems, recv_sems)
    z, zp, zm, z2, b = here.z, here.zp, here.zm, here.z2, here.b
    x, xp, xm, x2, a, c = here.x, here.xp, here.xm, here.x2, here.a, here.c
    micro, rows, width = x_ref.shape
    wr, wc = wg_ref.shape
    half_width = width // 2
    edge = width * 5 // 24
    m_blk = micro * rows
    n_blk = 2 * m_blk
    zs = {"o": z, "+": zp, "-": zm, "2": z2}
    xs_of = {"o": x, "+": xp, "-": xm, "2": x2}
    ring_z, ring_x = ("z+", "z-"), ("x+", "x-")

    def rows_at(start, size):
        return pl.ds(pl.multiple_of(start, size), size)

    weights_in = [Flag(24), Flag(24)]
    tokens_in = {k: Flag(5 if k == "o" else 6) for k in zs}
    ext_in = Flag(16)

    def up_slot(ref, core):
        return lambda q, p: ref.at[rows_at((q * 2 + core) * wr, wr), rows_at(p * wc, wc)]

    def down_slot(ref, core):
        return lambda q, p: ref.at[rows_at(p * wc, wc), rows_at((q * 2 + core) * wr, wr)]

    def row_half(ref, h):
        return nth(ref, h, 2)

    def tok_half(ref, h):
        return ref.at[h]

    in_z = (z, zp, zm, z2, b)
    in_x = (x, xp, xm, x2, a)

    def across(mine, theirs):
        def each(name, k, q, p):
            weights_in[k].hit()
            got, _ = net.send("core", mine(q, p), mine(q, p), theirs(q, p))
            net.arrive(got, weights_in[k])
        return each

    for fn, own, mine, theirs in (
        (gather_ring_first, wg_ref, up_slot(wg_all, c), up_slot(wg_all, 1 - c)),
        (functools.partial(gather_pair_first, late=True), wu_ref, up_slot(wu_all, c), up_slot(wu_all, 1 - c)),
        (functools.partial(gather_pair_first, late=True), wd_ref, down_slot(wd_all, c), down_slot(wd_all, 1 - c)),
    ):
        fn(net, own, mine, row_half, ring_x, "wgt", in_x, across(mine, theirs))
        got, _ = net.send("core", own, mine(x, a), theirs(x, a))
        net.arrive(got, weights_in[0])
        net.arrive(net.copy(own, mine(x, a)), weights_in[0])

    ext, ext_side = down_slot(wd_ext, c), down_slot(wd_ext, 1 - c)

    def ext_each(q, p):
        ext_in.hit()
        got, _ = net.send("core", ext(q, p), ext(q, p), ext_side(q, p))
        net.arrive(got, ext_in)

    def ext_round(p):
        from_down, _ = net.send("x+", ext(x, p), ext(x, p), ext(xm, p))
        from_up, _ = net.send("x-", ext(x, p), ext(x, p), ext(xp, p))
        far = []

        def near(q, h, link):
            def then():
                ref = row_half(ext(q, p), h)
                far.append(net.send(link, ref, ref, row_half(ext(x2, p), h))[0])
                ext_each(q, p)
                if len(far) == 2:
                    net.when(far, lambda: ext_each(x2, p))
            return then

        net.when([from_down], near(xm, 0, "x+"))
        net.when([from_up], near(xp, 1, "x-"))
        ext_each(x, p)

    def ext_start():
        got, _ = net.send("tok", wd_ref, ext(x, a))

        def pass_on():
            more, _ = net.send("wgt", ext(x, a), ext(x, a), ext(x, 1 - a))
            net.when([more], lambda: ext_round(1 - a))
            ext_round(a)

        net.when([got], pass_on)

    started = []

    def count_tokens(name, k, q, p):
        tokens_in[name].hit()

    def count_main(name, k, q, p):
        count_tokens(name, k, q, p)
        if name == "-" and not started:
            started.append(True)
            ext_start()

    for fn, own, dst, cols, each in (
        (gather_pair_first, x_ref, x_all, pl.ds(width - edge, edge), count_tokens),
        (gather_ring_first, x_ref, x_all, pl.ds(0, width - edge), count_main),
        (gather_pair_first, dy_ref, dy_all, pl.ds(0, width), count_tokens),
    ):
        slot = functools.partial(lambda q, p, dst, cols: dst.at[q, p, :, :, cols], dst=dst, cols=cols)
        fn(net, own.at[:, :, cols], slot, tok_half, ring_z, "tok", in_z, each)

    tok_pool = Pool([(xb.at[i], db.at[i]) for i in range(xb.shape[0])])
    cut_pool = Pool([(xs.at[i], ds.at[i]) for i in range(xs.shape[0])])
    r_pool = Pool([r_out.at[i] for i in range(r_out.shape[0])])
    q_pool = Pool([q_out.at[i] for i in range(q_out.shape[0])])
    y_pool = Pool([y_out.at[i] for i in range(y_out.shape[0])])
    ext_pool = Pool([wx.at[i] for i in range(wx.shape[0])])
    wout_pool = Pool([tw.at[i] for i in range(tw.shape[0])])
    tk_pool = Pool([tk.at[i] for i in range(tk.shape[0])])
    wk_pool = Pool([wk.at[i] for i in range(wk.shape[0])])

    first_slot = tok_pool.take(1)[0]
    bounce = tok_pool.refs[first_slot]
    into = [net.copy(src, ref.at[0]) for src, ref in zip((x_ref, dy_ref), bounce)]

    def own_rows():
        out = [net.copy(ref.at[0], dst.at[z, b]) for ref, dst in zip(bounce, (x_all, dy_all))]
        tok_pool.give(first_slot, out)
        for handle in out:
            net.arrive(handle, tokens_in["o"])

    net.when(into, own_rows)

    ranks = {step: 10 + i for i, step in enumerate(STEPS)}

    hidden = {k: Flag(2) for k in zs}
    ext_rows = Flag(4)
    tile_h = min(256, wc)

    def block(name):
        return rows_at(zs[name] * n_blk, n_blk)

    def hidden_of(name, turn):
        cols_at = a * wc if turn == 0 else (1 - a) * wc
        rank = ranks["H" + name + "ab"[turn]]
        loaded = Flag()
        held = []

        def load(slots):
            i = slots[0]
            held.append(i)
            one, two = tok_pool.refs[i]
            net.when([net.copy(x_all.at[zs[name]], one), net.copy(dy_all.at[zs[name]], two)], loaded.hit)

        def multiply():
            i = held[0]
            one, two = tok_pool.refs[i]
            at = block(name)

            @pl.loop(0, wc // tile_h)
            def _(j):
                cols = rows_at(cols_at + j * tile_h, tile_h)
                x_blk = one[...].reshape(n_blk, width)
                dy_blk = two[...].reshape(n_blk, width)
                pre = dot(x_blk, wg_all[:, cols], 1, 0)
                up = dot(x_blk, wu_all[:, cols], 1, 0)
                g = dot(dy_blk, wd_all[cols, :], 1, 1)
                s = jax.nn.sigmoid(pre)
                act = pre * s
                h_all[at, cols] = (act * up).astype(BF16)
                da_all[at, cols] = (g * up * s * (1.0 + pre * (1.0 - s))).astype(BF16)
                db_all[at, cols] = (g * act).astype(BF16)

            tok_pool.give(i)
            hidden[name].hit()

        net.job([tokens_in[name]], [(tok_pool, 1)], load, 0.1, rank * 0.01, "load")
        net.job([loaded, weights_in[turn]], [], multiply, 2.8, rank, "mxu")

    def give_hidden(name):
        def go():
            src = h_all.at[rows_at(zs[name] * n_blk + (1 - b) * m_blk, m_blk), :]
            got, _ = net.send("tok", src, h_ext.at[rows_at(zs[name] * m_blk, m_blk), :])
            net.arrive(got, ext_rows)
        net.job([hidden[name]], [], go, 0.1, 1)

    for name in zs:
        hidden_of(name, 0)
        hidden_of(name, 1)
        give_hidden(name)

    r_in = {k: Flag() for k in zs}
    q_in = {k: Flag() for k in zs}
    tile_dx = half_width // 2

    def rows_of(name, pool, part, flag, col0, rank):
        at = block(name)

        def multiply(slots):
            i = slots[0]
            ref = pool.refs[i]

            @pl.loop(0, half_width // tile_dx)
            def _(j):
                src = rows_at(col0 + j * tile_dx, tile_dx)
                val = dot(da_all[at, :], wg_all[src, :], 1, 1) + dot(db_all[at, :], wu_all[src, :], 1, 1)
                ref[:, :, :, rows_at(j * tile_dx, tile_dx)] = val.reshape(2, micro, rows, tile_dx)

            done = net.copy(ref, part.at[zs[name]])
            pool.give(i, [done])
            net.when([done], flag.hit)

        net.job([hidden[name]], [(pool, 1)], multiply, 1.9, rank, "mxu")

    for name in zs:
        rows_of(name, r_pool, r_pt, r_in[name], 0, ranks["R" + name])
        rows_of(name, q_pool, q_pt, q_in[name], half_width, ranks["Q" + name])

    quarter = width // 4
    tile_y = quarter // 3 if quarter % 3 == 0 else quarter
    y_in = [Flag(2), Flag(2)]

    def y_of(j):
        loaded = Flag()
        held = []
        cols = pl.ds(j * quarter, quarter)

        def load(slots):
            held.append(slots[0])
            net.when([net.copy(wd_ext.at[:, cols], ext_pool.refs[slots[0]])], loaded.hit)

        def multiply(slots):
            i = slots[0]
            ref = y_pool.refs[i]
            w_ref = ext_pool.refs[held[0]]
            mine = [rows_at(zs[name] * n_blk + b * m_blk, m_blk) for name in ORDER]
            other = [rows_at(zs[name] * m_blk, m_blk) for name in ORDER]

            @pl.loop(0, quarter // tile_y)
            def _(n):
                near = jnp.concatenate([h_all[at, :] for at in mine], axis=0)
                far = jnp.concatenate([h_ext[at, :] for at in other], axis=0)
                at = rows_at(n * tile_y, tile_y)
                val = dot(near, wd_all[:, rows_at(j * quarter + n * tile_y, tile_y)], 1, 0) + dot(far, w_ref[:, at], 1, 0)
                ref[:, :, :, at] = val.reshape(4, micro, rows, tile_y)

            ext_pool.give(held[0])
            half = pl.ds((j % 2) * quarter, quarter)
            out = [net.copy(ref.at[k], y_pt.at[j // 2, k, :, :, half]) for k in range(3)]
            out.append(net.copy(ref.at[3], y_own.at[:, :, cols]))
            y_pool.give(i, out)
            net.when(out, y_in[j // 2].hit)

        net.job([ext_in], [(ext_pool, 1)], load, 0.1, 3 + 0.01 * j, "ext")
        net.job([loaded, ext_rows], [(y_pool, 1)], multiply, 1.9, ranks["Y%d" % j], "mxu")

    for j in range(4):
        y_of(j)

    def tok_view(ref, shape):
        return ref if len(shape) == 3 else ref.at[0]

    tok_add = Adder(net, tk_pool, tok_view)
    names = {name: k for k, name in enumerate(ORDER)}

    r_near = [Flag(2), Flag(2)]
    ring_reduce(
        net, tok_add, lambda name, h: [r_in[name]], lambda name, h: [r_pt.at[zs[name], :, h]],
        r_l1, r_l2, ring_z, r_near,
    )

    def r_last(h):
        away = r_pt.at[z, 1 - b, h]

        def go():
            got, _ = net.send("tok", away, r_lp.at[h])
            net.when([got], nothing)

        tok_add.add(
            [r_in["o"], r_near[h]], [r_pt.at[z, :, h], r_l2.at[0, h], r_l2.at[1, h]],
            lambda ref: [(ref.at[1 - b], away), (ref.at[b], r_own.at[h])], go,
        )

    r_last(0)
    r_last(1)

    for j in range(2):
        ring_reduce(
            net, tok_add, lambda name, h, j=j: [y_in[j]], lambda name, h, j=j: [y_pt.at[j, names[name], h]],
            y_l1.at[j], y_l2.at[j], ring_z, [Flag(2), Flag(2)],
        )

    q_pair = {k: Flag() for k in zs}

    def pair_q(name):
        def go():
            got, _ = net.send("tok", q_pt.at[zs[name], 1 - b], q_lp.at[names[name]])
            net.arrive(got, q_pair[name])
        net.job([q_in[name]], [], go, 0.1, 1)

    for name in ORDER:
        pair_q(name)
    ring_reduce(
        net, tok_add, lambda name, h: [q_in[name], q_pair[name]],
        lambda name, h: [q_pt.at[zs[name], b, h], q_lp.at[names[name], h]], q_l1, q_l2, ring_z, [Flag(2), Flag(2)],
    )
    tok_add.add(
        [q_in["o"], q_pair["o"]], [q_pt.at[z, b], q_lp.at[3]], lambda ref: [(ref, q_own)], nothing,
    )

    tile_w = wc
    n_tok = 4 * n_blk
    w_in = {(m, k): Flag() for m in range(3) for k in range(4)}
    w_side = {(m, k): Flag() for m in range(3) for k in range(4)}
    all_hidden = list(hidden.values())

    def grads_of(k, name, core, turn):
        loaded = Flag()
        held = []
        cols = rows_at((xs_of[name] * 2 + core) * wr, wr)

        def load(slots):
            i = slots[0]
            held.append(i)
            one, two = cut_pool.refs[i]
            net.when([net.copy(x_all.at[:, :, :, :, cols], one), net.copy(dy_all.at[:, :, :, :, cols], two)], loaded.hit)

        def out(m, j, ref):
            if turn == 0:
                got, sent = net.send("core", ref, w_lc.at[m, k])
                wout_pool.give(j, [sent])
                net.arrive(got, w_side[m, k])
            else:
                done = net.copy(ref, w_pt.at[m, k])
                wout_pool.give(j, [done])
                net.when([done], w_in[m, k].hit)

        def from_x(slots):
            one, _ = cut_pool.refs[held[0]]
            outs = [wout_pool.refs[j] for j in slots]

            @pl.loop(0, 2 * wc // tile_w)
            def _(j):
                at = rows_at(j * tile_w, tile_w)
                cut = one[...].reshape(n_tok, wr)
                outs[0][:, at] = dot(cut, da_all[:, at], 0, 0)
                outs[1][:, at] = dot(cut, db_all[:, at], 0, 0)

            for m in range(2):
                out(m, slots[m], outs[m])

        def from_dy(slots):
            _, two = cut_pool.refs[held[0]]
            ref = wout_pool.refs[slots[0]]

            @pl.loop(0, 2 * wc // tile_w)
            def _(j):
                at = rows_at(j * tile_w, tile_w)
                ref[:, at] = dot(two[...].reshape(n_tok, wr), h_all[:, at], 0, 0)

            cut_pool.give(held[0])
            out(2, slots[0], ref)

        rank = ranks["W%d%s" % (k, "ab"[turn])]
        net.job(list(tokens_in.values()), [(cut_pool, 1)], load, 0.1, 2 + 0.01 * rank, "cut")
        net.job([loaded] + all_hidden, [(wout_pool, 2)], from_x, 2.0, rank, "mxu")
        net.job([loaded] + all_hidden, [(wout_pool, 1)], from_dy, 1.1, rank + 0.5, "mxu")

    for k, name in enumerate(ORDER):
        grads_of(k, name, 1 - c, 0)
        grads_of(k, name, c, 1)

    def w_view(ref, shape):
        return ref.at[pl.ds(0, shape[0]), pl.ds(0, shape[1])]

    w_add = Adder(net, wk_pool, w_view)
    mine, other = rows_at(a * wc, wc), rows_at((1 - a) * wc, wc)

    def w_ring_first(m, row0, size, l1, l2, lp, own):
        def part(ref, h):
            return ref.at[pl.ds(row0 + h * (size // 2), size // 2)]

        near = [Flag(2), Flag(2)]
        ring_reduce(
            net, w_add, lambda name, h: [w_in[m, names[name]], w_side[m, names[name]]],
            lambda name, h: [part(w_pt.at[m, names[name]], h), part(w_lc.at[m, names[name]], h)], l1, l2, ring_x, near,
        )

        def last(h):
            block = part(w_pt.at[m, 3], h)
            away = block.at[:, other]

            def go():
                got, _ = net.send("wgt", away, row_half(lp, h))
                net.when([got], nothing)

            w_add.add(
                [w_in[m, 3], w_side[m, 3], near[h]], [block, part(w_lc.at[m, 3], h), l2.at[0, h], l2.at[1, h]],
                lambda ref: [(ref.at[:, other], away), (ref.at[:, mine], row_half(own, h))], go,
            )

        last(0)
        last(1)

    def w_pair_first(m, row0, size, lp, l1, l2, own):
        def part(ref, h):
            return ref.at[pl.ds(row0 + h * (size // 2), size // 2)]

        have = {k: [w_in[m, k], w_side[m, k]] for k in range(4)}
        pair = {(k, h): Flag() for k in range(4) for h in range(2)}

        def away(k, h):
            dst = part(w_pt.at[m, k], h).at[:, other]

            def go():
                got, _ = net.send("wgt", dst, row_half(lp.at[k], h))
                net.arrive(got, pair[k, h])

            w_add.add(have[k], [dst, part(w_lc.at[m, k], h).at[:, other]], lambda ref: [(ref, dst)], go)

        for k in range(4):
            for h in range(2):
                away(k, h)

        def terms(name, h):
            k = names[name]
            return [part(w_pt.at[m, k], h).at[:, mine], part(w_lc.at[m, k], h).at[:, mine], row_half(lp.at[k], h)]

        def ready(name, h):
            return have[names[name]] + [pair[names[name], h]]

        ring_reduce(net, w_add, ready, terms, l1, l2, ring_x, [Flag(2), Flag(2)])
        for h in range(2):
            w_add.add(ready("o", h), terms("o", h), lambda ref, h=h: [(ref, row_half(own, h))], nothing)

    most = wr * 2 // 3
    w_ring_first(0, 0, wr, g_l1, g_l2, g_lp, g_own)
    w_pair_first(2, 0, wr, d_lp, d_l1, d_l2, d_own)
    w_ring_first(1, 0, most, u_l1, u_l2, u_lp, u_own)
    w_pair_first(1, most, wr - most, v_lp, v_l1, v_l2, v_own)
    net.run()


def solution(mesh):
    row_spec = P(None, ("dp", "tp"), None)
    in_specs = (row_spec, P("dp", "tp"), P("dp", "tp"), P("tp", "dp"), row_spec)
    out_specs = (row_spec, row_spec, P("dp", "tp"), P("dp", "tp"), P("tp", "dp"))
    hbm = pl.BlockSpec(memory_space=pl.ANY)
    dma = pltpu.SemaphoreType.DMA
    V = pltpu.VMEM
    S = jax.ShapeDtypeStruct

    def local_step(x_loc, wg, wu, wd, dy_loc):
        micro, rows, width = x_loc.shape
        wr, wc = wg.shape
        half = width // 2
        most = wr * 2 // 3
        tok = (micro, rows, width)
        tok_h = (micro, rows, half)
        n = 8 * micro * rows

        def ring_first(size):
            return S((2, size // 2, 2 * wc), F32), S((2, 2, size // 2, 2 * wc), F32)

        def pair_first(size):
            return S((4, size, wc), F32), S((2, size // 2, wc), F32)

        def pair_last(size):
            return S((size, wc), F32), S((2, 2, size // 2, wc), F32)

        outs = [
            S(tok, F32), S((2, 2) + tok_h, F32), S(tok_h, F32), S(tok_h, F32), S(tok_h, F32), S((2,) + tok_h, F32),
            S((wr, wc), F32), S((wr, wc), F32), S((most, wc), F32), S((most, wc), F32),
            *pair_last(wr - most), *pair_last(wr),
        ]
        space = [
            S((4, 2) + tok, BF16), S((4, 2) + tok, BF16), S((2 * wc, width), BF16),
            S((2, 3) + tok_h, F32), S((4, 2) + tok_h, F32), S((4, 2) + tok_h, F32), S((3, 4, wr, 2 * wc), F32),
            S((2, 2) + tok_h[1:], F32), S((2, 2) + tok_h[1:], F32), S((2, 2, 2) + tok_h[1:], F32),
            S((4,) + tok_h, F32), S((2,) + tok_h[1:], F32), S((3, 4, wr, 2 * wc), F32),
            *ring_first(wr), *ring_first(most), *pair_first(wr - most), *pair_first(wr),
        ]
        res = pl.pallas_call(
            layer_kernel,
            name="layer",
            out_shape=tuple(outs + space),
            in_specs=[hbm] * 5,
            out_specs=[hbm] * (len(outs) + len(space)),
            scratch_shapes=[
                V((width, 2 * wc), BF16), V((width, 2 * wc), BF16), V((2 * wc, width), BF16),
                V((n, 2 * wc), BF16), V((n, 2 * wc), BF16), V((n, 2 * wc), BF16), V((n // 2, 2 * wc), BF16),
                V((2, 2) + tok, BF16), V((2, 2) + tok, BF16),
                V((2, 4, 2, micro, rows, wr), BF16), V((2, 4, 2, micro, rows, wr), BF16),
                V((1, 2) + tok_h, F32), V((2, 2) + tok_h, F32),
                V((2, 4, micro, rows, width // 4), F32), V((2, 2 * wc, width // 4), BF16), V((5, wr, 2 * wc), F32),
                V((6, 2, rows, half), F32), V((6, wr // 2, 2 * wc), F32),
                dma((128,)), dma((200,)), dma((200,)),
            ],
            compiler_params=pltpu.CompilerParams(
                collective_id=0, has_side_effects=True, vmem_limit_bytes=67_000_000
            ),
        )(x_loc, dy_loc, wg, wu, wd)
        y_own, y_l2, r_own, r_lp, q_own, q_l2, g_own, g_lp, u_own, u_lp, v_own, v_l2, d_own, d_l2 = res[: len(outs)]
        y_in = jnp.concatenate([y_l2[j, 0] + y_l2[j, 1] for j in range(2)], axis=2)
        y = (x_loc.astype(F32) + (y_own + y_in)).astype(BF16)
        dx = (dy_loc.astype(F32) + jnp.concatenate([r_own + r_lp, q_own + q_l2[0] + q_l2[1]], axis=2)).astype(BF16)
        u_sum = jnp.concatenate([u_own + u_lp, v_own + (v_l2[0] + v_l2[1]).reshape(v_own.shape)], axis=0)
        d_sum = d_own + (d_l2[0] + d_l2[1]).reshape(d_own.shape)
        return y, dx, g_own + g_lp, u_sum, d_sum.T

    return jax.shard_map(local_step, mesh=mesh, in_specs=in_specs, out_specs=out_specs, check_vma=False)
```

time: 280 us -> 262 us (0.936)
  Pallas kernels: 266 us -> 244 us
  other arithmetic: 5.8 us -> 9.21 us
    pallas_call x1, Pallas kernels: 266 us -> 244 us  [local_step(): pl.pallas_call(layer_kernel, name='layer', out_shape=tuple(outs + space),...]
    add x4 -> x9, other arithmetic: 4.23 us -> 6.59 us  [the longest x2 1.19 us: local_step(): d_sum = d_own + (d_l2[0] + d_l2[1]).reshape(d_own.shape)]
    unnamed x17 -> x33, local copies, waits for them, and re-layouts: 5.27 us -> 7.52 us
where the time goes in v2:
time: 262 us; the launch traced here: 261 us
  Pallas kernels  244 us (93%)
  other arithmetic  9.21 us (4%)
  local copies, waits for them, and re-layouts  7.52 us (3%)
    pallas_call x1, Pallas kernels, local_step(): pl.pallas_call(layer_kernel, name='layer', out_shape=tuple(outs + space),...  244 us
    unnamed x33, local copies, waits for them, and re-layouts  7.52 us

profile of v2, /device:TPU:1, one launch (start us, length us, event | category | flops | bytes accessed | tf_op | source)
XLA Modules:
  0.0 261.2 jit_solution(13583779661657110930)
XLA Ops:
  0.6 243.7 %layer.1 = (f32[2,64,3072]{2,1,0:T(8,128)}, f32[2,2,2,64,1536]{4,3,2,1,0:T(8,128)}, f32[2,64,1536]{2,1,0:T(8,128)}, f32[2,64,1536]{2,1,0:T(8,128)}, f32[2,64,153...) custom-call(bf16[2,64,3072]{2,1,0:T(8,128)(2,1)} %x_ref.1, ...), custom_call_target="tpu_custom_call" | custom-call | tf_op jit(solution)/shard_map/layer/pallas_call | solution.py:854
  244.3 1.2 slice_add_fusion.1
  245.5 1.0 bitcast_add_fusion.3
  246.5 0.1 add.67
  246.6 0.9 pad_maximum_fusion
  247.6 0.2 copy-done.12
  247.7 0.4 copy-done.13
  248.1 1.0 add.62
  249.1 1.0 bitcast_add_fusion.1
  250.1 0.3 copy-done.9
  250.5 0.3 copy-done.10
  250.8 1.0 add.66
  251.8 0.7 copy-done.5
  252.5 0.1 slice_add_fusion
  252.6 1.0 copy-done.8
  253.6 1.1 bitcast_add_fusion
  254.7 2.5 copy.10
  257.1 0.2 add_bitcast_fusion.1
  257.3 0.9 copy-done.1
  258.2 0.2 copy-done.2
  258.5 0.2 copy-done.3
  258.7 0.2 copy-done.4
  259.0 0.5 copy-done.7
  259.5 1.7 fusion.1
  (21 shorter events, 0.0 us)
Async XLA Ops:
  244.3 2.2 copy-start.14
  244.3 2.2 copy-start.15
  246.5 1.2 copy-start.12
  246.5 1.6 copy-start.13
  246.6 2.5 copy-start.6
  246.6 2.5 copy-start.11
  249.1 1.3 copy-start.9
  249.1 1.7 copy-start.10
  250.8 1.7 copy-start.5
  252.5 1.1 copy-start.8
  253.6 3.5 %copy-start = (f32[2,2,2,64,1536]{4,3,2,1,0:T(8,128)S(1)}, f32[2,2,2,64,1536]{4,3,2,1,0:T(8,128)}, u32[]{:S(2)}) copy-start(f32[2,2,2,64,1536]{4,3,2,1,0:T(8,128)} %get-tuple-element.20) | copy-start | bytes 9437188
  257.1 1.1 copy-start.1
  257.1 1.4 copy-start.2
  257.1 1.6 copy-start.3
  257.1 1.8 copy-start.4
  257.1 2.3 copy-start.7

commit v3 on v2

--- a/solution.py
+++ b/solution.py
@@ -14,11 +14,19 @@
 ICI_RATE = 45.0e3
 CORE_RATE = 550.0e3
 HBM_RATE = 2.5e6
-MARGIN = 1.0
+MARGIN = 0.5
+FIRST, NEXT, EARLY = 0.5, 1, 0.01
+SIDES = (0, 1)
+RING = 4
+AROUND = (1, 3, 2)
+BLOCKS = {
+    "A": (("o", 0), ("o", 1)), "B": (("-", 0), ("+", 0)), "C": (("-", 1), ("+", 1)), "D": (("2", 0),), "E": (("2", 1),),
+}
 STEPS = (
-    "Hoa", "H-a", "Hob", "H-b", "H+b", "R-", "H+a", "H2b", "H2a", "R2",
-    "W0a", "W0b", "Q2", "Y0", "Y2", "R+", "W2a", "W2b", "W1a", "W3a",
-    "W1b", "Ro", "Q-", "Y1", "Y3", "Q+", "Qo", "W3b",
+    "HAa", "HBa", "HBb", "HAb", "HDb", "HCb", "HCa", "HDa", "HEb", "HEa",
+    "R2", "W0au", "W0ad", "W0bu", "W0bd", "R+", "W0bg", "W0ag", "W2a", "R-",
+    "Q+", "Q2", "W2b", "W1a", "W3b", "Y2", "W1b", "Y0", "Y1", "Qo",
+    "Q-", "Ro", "W3a", "Y3",
 )
 
 
@@ -33,15 +41,15 @@
     def __init__(self):
         t = lax.axis_index("tp")
         d = lax.axis_index("dp")
-        z, y, x, c = t // 4, t % 4, d // 2, d % 2
+        z, y, x, c = t // RING, t % RING, d // 2, d % 2
         self.z, self.y, self.x, self.c = z, y, x, c
         self.b = y % 2
         self.a = y // 2
-        self.zp, self.zm, self.z2 = (z + 1) % 4, (z + 3) % 4, (z + 2) % 4
-        self.xp, self.xm, self.x2 = (x + 1) % 4, (x + 3) % 4, (x + 2) % 4
+        self.zp, self.zm, self.z2 = ((z + n) % RING for n in AROUND)
+        self.xp, self.xm, self.x2 = ((x + n) % RING for n in AROUND)
 
         def at(z, y, x, c):
-            return {"tp": z * 4 + y, "dp": x * 2 + c}
+            return {"tp": z * RING + y, "dp": x * 2 + c}
 
         self.dev = {
             "z+": at(self.zp, y, x, c),
@@ -161,7 +169,7 @@
         self.seq += 1
         heapq.heappush(self.heap, (max(h.time for h in handles), self.seq, handles, then))
 
-    def job(self, flags, needs, then, cost, rank, line=None):
+    def job(self, flags, needs, then, rank, line=None, cost=0.1):
         self.seq += 1
         self.jobs.append((rank, self.seq, flags, needs, then, cost, line))
         self.jobs.sort(key=lambda j: j[:2])
@@ -339,7 +347,7 @@
 
             net.when(loads, done)
 
-        net.job(flags, [(pool, len(srcs))], begin, 0.1, 1)
+        net.job(flags, [(pool, len(srcs))], begin, NEXT)
 
 
 def ring_reduce(net, adder, ready, srcs, l1, l2, links, near):
@@ -353,7 +361,7 @@
             net.arrive(got, flag)
 
         if len(terms) == 1:
-            net.job(ready(name, h) + flags, [], send, 0.1, 1)
+            net.job(ready(name, h) + flags, [], send, NEXT)
         else:
             adder.add(ready(name, h) + flags, terms, lambda ref: [(ref, terms[0])], send)
 
@@ -391,7 +399,8 @@
         return pl.ds(pl.multiple_of(start, size), size)
 
     weights_in = [Flag(24), Flag(24)]
-    tokens_in = {k: Flag(5 if k == "o" else 6) for k in zs}
+    pieces = [(name, side) for name in zs for side in range(2)]
+    tokens_in = {piece: Flag(2 if piece == ("o", 0) else 3) for piece in pieces}
     ext_in = Flag(16)
 
     def up_slot(ref, core):
@@ -464,7 +473,7 @@
     started = []
 
     def count_tokens(name, k, q, p):
-        tokens_in[name].hit()
+        tokens_in[name, k].hit()
 
     def count_main(name, k, q, p):
         count_tokens(name, k, q, p)
@@ -498,66 +507,78 @@
         out = [net.copy(ref.at[0], dst.at[z, b]) for ref, dst in zip(bounce, (x_all, dy_all))]
         tok_pool.give(first_slot, out)
         for handle in out:
-            net.arrive(handle, tokens_in["o"])
+            net.arrive(handle, tokens_in["o", 0])
 
     net.when(into, own_rows)
 
     ranks = {step: 10 + i for i, step in enumerate(STEPS)}
 
-    hidden = {k: Flag(2) for k in zs}
+    hidden = {piece: Flag(2) for piece in pieces}
     ext_rows = Flag(4)
     tile_h = min(256, wc)
 
-    def block(name):
-        return rows_at(zs[name] * n_blk, n_blk)
-
-    def hidden_of(name, turn):
+    def piece_rows(piece):
+        name, side = piece
+        return rows_at(zs[name] * n_blk + (b if side == 0 else 1 - b) * m_blk, m_blk)
+
+    def hidden_of(key, turn):
+        block = BLOCKS[key]
+        count = len(block)
         cols_at = a * wc if turn == 0 else (1 - a) * wc
-        rank = ranks["H" + name + "ab"[turn]]
+        rank = ranks["H" + key + "ab"[turn]]
         loaded = Flag()
         held = []
 
         def load(slots):
             i = slots[0]
             held.append(i)
-            one, two = tok_pool.refs[i]
-            net.when([net.copy(x_all.at[zs[name]], one), net.copy(dy_all.at[zs[name]], two)], loaded.hit)
+            copies = []
+            for n, (name, side) in enumerate(block):
+                for ref, src in zip(tok_pool.refs[i], (x_all, dy_all)):
+                    copies.append(net.copy(src.at[zs[name], b if side == 0 else 1 - b], ref.at[n]))
+            net.when(copies, loaded.hit)
 
         def multiply():
             i = held[0]
             one, two = tok_pool.refs[i]
-            at = block(name)
 
             @pl.loop(0, wc // tile_h)
             def _(j):
                 cols = rows_at(cols_at + j * tile_h, tile_h)
-                x_blk = one[...].reshape(n_blk, width)
-                dy_blk = two[...].reshape(n_blk, width)
+                x_blk = one[:count].reshape(count * m_blk, width)
+                dy_blk = two[:count].reshape(count * m_blk, width)
                 pre = dot(x_blk, wg_all[:, cols], 1, 0)
                 up = dot(x_blk, wu_all[:, cols], 1, 0)
                 g = dot(dy_blk, wd_all[cols, :], 1, 1)
                 s = jax.nn.sigmoid(pre)
                 act = pre * s
-                h_all[at, cols] = (act * up).astype(BF16)
-                da_all[at, cols] = (g * up * s * (1.0 + pre * (1.0 - s))).astype(BF16)
-                db_all[at, cols] = (g * act).astype(BF16)
+                h = (act * up).astype(BF16)
+                da = (g * up * s * (1.0 + pre * (1.0 - s))).astype(BF16)
+                db = (g * act).astype(BF16)
+                for n, piece in enumerate(block):
+                    at = piece_rows(piece)
+                    cut = slice(n * m_blk, (n + 1) * m_blk)
+                    h_all[at, cols] = h[cut]
+                    da_all[at, cols] = da[cut]
+                    db_all[at, cols] = db[cut]
 
             tok_pool.give(i)
-            hidden[name].hit()
-
-        net.job([tokens_in[name]], [(tok_pool, 1)], load, 0.1, rank * 0.01, "load")
-        net.job([loaded, weights_in[turn]], [], multiply, 2.8, rank, "mxu")
+            for piece in block:
+                hidden[piece].hit()
+
+        net.job([tokens_in[piece] for piece in block], [(tok_pool, 1)], load, rank * EARLY, "load")
+        net.job([loaded, weights_in[turn]], [], multiply, rank, "mxu", 1.2 + 0.8 * count)
 
     def give_hidden(name):
         def go():
-            src = h_all.at[rows_at(zs[name] * n_blk + (1 - b) * m_blk, m_blk), :]
-            got, _ = net.send("tok", src, h_ext.at[rows_at(zs[name] * m_blk, m_blk), :])
+            got, _ = net.send("tok", h_all.at[piece_rows((name, 1)), :], h_ext.at[rows_at(zs[name] * m_blk, m_blk), :])
             net.arrive(got, ext_rows)
-        net.job([hidden[name]], [], go, 0.1, 1)
-
+        net.job([hidden[name, 1]], [], go, NEXT)
+
+    for key in BLOCKS:
+        hidden_of(key, 0)
+        hidden_of(key, 1)
     for name in zs:
-        hidden_of(name, 0)
-        hidden_of(name, 1)
         give_hidden(name)
 
     r_in = {k: Flag() for k in zs}
@@ -565,7 +586,7 @@
     tile_dx = half_width // 2
 
     def rows_of(name, pool, part, flag, col0, rank):
-        at = block(name)
+        at = rows_at(zs[name] * n_blk, n_blk)
 
         def multiply(slots):
             i = slots[0]
@@ -581,7 +602,7 @@
             pool.give(i, [done])
             net.when([done], flag.hit)
 
-        net.job([hidden[name]], [(pool, 1)], multiply, 1.9, rank, "mxu")
+        net.job([hidden[name, side] for side in SIDES], [(pool, 1)], multiply, rank, "mxu", 2.0)
 
     for name in zs:
         rows_of(name, r_pool, r_pt, r_in[name], 0, ranks["R" + name])
@@ -622,8 +643,9 @@
             y_pool.give(i, out)
             net.when(out, y_in[j // 2].hit)
 
-        net.job([ext_in], [(ext_pool, 1)], load, 0.1, 3 + 0.01 * j, "ext")
-        net.job([loaded, ext_rows], [(y_pool, 1)], multiply, 1.9, ranks["Y%d" % j], "mxu")
+        net.job([ext_in], [(ext_pool, 1)], load, ranks["Y%d" % j] * EARLY, "ext")
+        own = [hidden[name, 0] for name in zs]
+        net.job([loaded, ext_rows] + own, [(y_pool, 1)], multiply, ranks["Y%d" % j], "mxu", 2.1)
 
     for j in range(4):
         y_of(j)
@@ -667,7 +689,7 @@
         def go():
             got, _ = net.send("tok", q_pt.at[zs[name], 1 - b], q_lp.at[names[name]])
             net.arrive(got, q_pair[name])
-        net.job([q_in[name]], [], go, 0.1, 1)
+        net.job([q_in[name]], [], go, NEXT)
 
     for name in ORDER:
         pair_q(name)
@@ -684,6 +706,7 @@
     w_in = {(m, k): Flag() for m in range(3) for k in range(4)}
     w_side = {(m, k): Flag() for m in range(3) for k in range(4)}
     all_hidden = list(hidden.values())
+    mats = range(3)
 
     def grads_of(k, name, core, turn):
         loaded = Flag()
@@ -701,41 +724,53 @@
                 got, sent = net.send("core", ref, w_lc.at[m, k])
                 wout_pool.give(j, [sent])
                 net.arrive(got, w_side[m, k])
-            else:
-                done = net.copy(ref, w_pt.at[m, k])
-                wout_pool.give(j, [done])
-                net.when([done], w_in[m, k].hit)
-
-        def from_x(slots):
-            one, _ = cut_pool.refs[held[0]]
-            outs = [wout_pool.refs[j] for j in slots]
-
-            @pl.loop(0, 2 * wc // tile_w)
-            def _(j):
-                at = rows_at(j * tile_w, tile_w)
-                cut = one[...].reshape(n_tok, wr)
-                outs[0][:, at] = dot(cut, da_all[:, at], 0, 0)
-                outs[1][:, at] = dot(cut, db_all[:, at], 0, 0)
-
-            for m in range(2):
-                out(m, slots[m], outs[m])
-
-        def from_dy(slots):
-            _, two = cut_pool.refs[held[0]]
-            ref = wout_pool.refs[slots[0]]
-
-            @pl.loop(0, 2 * wc // tile_w)
-            def _(j):
-                at = rows_at(j * tile_w, tile_w)
-                ref[:, at] = dot(two[...].reshape(n_tok, wr), h_all[:, at], 0, 0)
-
-            cut_pool.give(held[0])
-            out(2, slots[0], ref)
-
-        rank = ranks["W%d%s" % (k, "ab"[turn])]
-        net.job(list(tokens_in.values()), [(cut_pool, 1)], load, 0.1, 2 + 0.01 * rank, "cut")
-        net.job([loaded] + all_hidden, [(wout_pool, 2)], from_x, 2.0, rank, "mxu")
-        net.job([loaded] + all_hidden, [(wout_pool, 1)], from_dy, 1.1, rank + 0.5, "mxu")
+                return
+
+            def begin(slots):
+                halves = [(nth(ref, h, 2), wk_pool.refs[i]) for h, i in enumerate(slots)]
+                loads = [net.copy(nth(w_lc.at[m, k], h, 2), slot) for h, (_, slot) in enumerate(halves)]
+
+                def add():
+                    for i, (dst, slot) in zip(slots, halves):
+                        sum_rows(dst, [slot])
+                        wk_pool.give(i)
+                    net.now += 0.8
+                    done = net.copy(ref, w_pt.at[m, k])
+                    wout_pool.give(j, [done])
+                    net.when([done], w_in[m, k].hit)
+
+                net.when(loads, add)
+
+            net.job([w_side[m, k]], [(wk_pool, 2)], begin, FIRST)
+
+        def multiply(which, free):
+            def then(slots):
+                refs = [wout_pool.refs[j] for j in slots]
+                one, two = cut_pool.refs[held[0]]
+
+                @pl.loop(0, 2 * wc // tile_w)
+                def _(j):
+                    at = rows_at(j * tile_w, tile_w)
+                    for m, ref in zip(which, refs):
+                        cut = (two if m == 2 else one)[...].reshape(n_tok, wr)
+                        ref[:, at] = dot(cut, (da_all, db_all, h_all)[m][:, at], 0, 0)
+
+                if free:
+                    cut_pool.give(held[0])
+                for m, j, ref in zip(which, slots, refs):
+                    out(m, j, ref)
+            return then
+
+        flags = [loaded] + all_hidden
+        step = "W%d%s" % (k, "ab"[turn])
+        first = min(ranks[step + m] for m in "gud") if k == 0 else ranks[step]
+        net.job(list(tokens_in.values()), [(cut_pool, 1)], load, first * EARLY, "cut")
+        if k == 0:
+            last = max(mats, key=lambda m: ranks[step + "gud"[m]])
+            for m in range(3):
+                net.job(flags, [(wout_pool, 1)], multiply([m], m == last), ranks[step + "gud"[m]], "mxu", 1.15)
+        else:
+            net.job(flags, [(wout_pool, len(mats))], multiply(mats, True), ranks[step], "mxu", 2.8)
 
     for k, name in enumerate(ORDER):
         grads_of(k, name, 1 - c, 0)
@@ -753,8 +788,8 @@
 
         near = [Flag(2), Flag(2)]
         ring_reduce(
-            net, w_add, lambda name, h: [w_in[m, names[name]], w_side[m, names[name]]],
-            lambda name, h: [part(w_pt.at[m, names[name]], h), part(w_lc.at[m, names[name]], h)], l1, l2, ring_x, near,
+            net, w_add, lambda name, h: [w_in[m, names[name]]],
+            lambda name, h: [part(w_pt.at[m, names[name]], h)], l1, l2, ring_x, near,
         )
 
         def last(h):
@@ -766,7 +801,7 @@
                 net.when([got], nothing)
 
             w_add.add(
-                [w_in[m, 3], w_side[m, 3], near[h]], [block, part(w_lc.at[m, 3], h), l2.at[0, h], l2.at[1, h]],
+                [w_in[m, 3], near[h]], [block, l2.at[0, h], l2.at[1, h]],
                 lambda ref: [(ref.at[:, other], away), (ref.at[:, mine], row_half(own, h))], go,
             )
 
@@ -777,17 +812,15 @@
         def part(ref, h):
             return ref.at[pl.ds(row0 + h * (size // 2), size // 2)]
 
-        have = {k: [w_in[m, k], w_side[m, k]] for k in range(4)}
+        have = {k: [w_in[m, k]] for k in range(4)}
         pair = {(k, h): Flag() for k in range(4) for h in range(2)}
 
         def away(k, h):
-            dst = part(w_pt.at[m, k], h).at[:, other]
-
             def go():
-                got, _ = net.send("wgt", dst, row_half(lp.at[k], h))
+                got, _ = net.send("wgt", part(w_pt.at[m, k], h).at[:, other], row_half(lp.at[k], h))
                 net.arrive(got, pair[k, h])
 
-            w_add.add(have[k], [dst, part(w_lc.at[m, k], h).at[:, other]], lambda ref: [(ref, dst)], go)
+            net.job(have[k], [], go, NEXT)
 
         for k in range(4):
             for h in range(2):
@@ -795,7 +828,7 @@
 
         def terms(name, h):
             k = names[name]
-            return [part(w_pt.at[m, k], h).at[:, mine], part(w_lc.at[m, k], h).at[:, mine], row_half(lp.at[k], h)]
+            return [part(w_pt.at[m, k], h).at[:, mine], row_half(lp.at[k], h)]
 
         def ready(name, h):
             return have[names[name]] + [pair[names[name], h]]
@@ -810,6 +843,60 @@
     w_ring_first(1, 0, most, u_l1, u_l2, u_lp, u_own)
     w_pair_first(1, most, wr - most, v_lp, v_l1, v_l2, v_own)
     net.run()
+
+
+def finish_kernel(
+    x_ref, dy_ref, y_own, y_l2, r_own, r_lp, q_own, q_l2, g_own, g_lp, u_own, u_lp, v_own, v_l2, d_own, d_l2,
+    y_ref, dx_ref, g_ref, u_ref, d_ref,
+):
+    i = pl.program_id(0)
+    half = r_own.shape[-1]
+    for j in range(2):
+        cols = pl.ds(j * half, half)
+        total = y_own[:, :, cols] + y_l2[j, 0] + y_l2[j, 1]
+        y_ref[:, :, cols] = (x_ref[:, :, cols].astype(F32) + total).astype(BF16)
+    low, high = pl.ds(0, half), pl.ds(half, half)
+    dx_ref[:, :, low] = (dy_ref[:, :, low].astype(F32) + (r_own[...] + r_lp[...])).astype(BF16)
+    dx_ref[:, :, high] = (dy_ref[:, :, high].astype(F32) + (q_own[...] + q_l2[0] + q_l2[1])).astype(BF16)
+    g_ref[...] = g_own[...] + g_lp[...]
+    most, size, rest = u_own.shape[0] * pl.num_programs(0), u_own.shape[0], v_own.shape[0]
+    u_ref[pl.ds(pl.multiple_of(i * size, size), size), :] = u_own[...] + u_lp[...]
+    u_ref[pl.ds(pl.multiple_of(4 * size + i * rest, rest), rest), :] = v_own[...] + v_l2[0, 0] + v_l2[1, 0]
+    rows, cols = d_own.shape
+    total = d_own[...] + d_l2[0].reshape(rows, cols) + d_l2[1].reshape(rows, cols)
+    d_ref[...] = total.T
+
+
+def finish(x, dy, y_own, y_l2, r_own, r_lp, q_own, q_l2, g_own, g_lp, u_own, u_lp, v_own, v_l2, d_own, d_l2):
+    micro, rows, width = x.shape
+    wr, wc = g_own.shape
+    half = width // 2
+    n = 4
+    B = pl.BlockSpec
+    S = jax.ShapeDtypeStruct
+
+    def tok(cols):
+        return B((micro, rows // n, cols), lambda i: (0, i, 0))
+
+    def flat(rows, cols):
+        return B((rows // n, cols), lambda i: (i, 0))
+
+    most, rest = u_own.shape[0], v_own.shape[0]
+    return pl.pallas_call(
+        finish_kernel,
+        name="finish",
+        grid=(n,),
+        out_shape=(S(x.shape, BF16), S(x.shape, BF16), S((wr, wc), F32), S((wr, wc), F32), S((wc, wr), F32)),
+        in_specs=[
+            tok(width), tok(width), tok(width), B((2, 2, micro, rows // n, half), lambda i: (0, 0, 0, i, 0)),
+            tok(half), tok(half), tok(half), B((2, micro, rows // n, half), lambda i: (0, 0, i, 0)),
+            flat(wr, wc), flat(wr, wc), flat(most, wc), flat(most, wc),
+            flat(rest, wc), B((2, 1, rest // n, wc), lambda i: (0, i // 2, i % 2, 0)),
+            B((wr, wc // n), lambda i: (0, i)), B((2, 2, wr // 2, wc // n), lambda i: (0, 0, 0, i)),
+        ],
+        out_specs=[tok(width), tok(width), flat(wr, wc), B((wr, wc), lambda i: (0, 0)), B((wc // n, wr), lambda i: (i, 0))],
+        compiler_params=pltpu.CompilerParams(vmem_limit_bytes=60 * 2**20),
+    )(x, dy, y_own, y_l2, r_own, r_lp, q_own, q_l2, g_own, g_lp, u_own, u_lp, v_own, v_l2, d_own, d_l2)
 
 
 def solution(mesh):
@@ -824,6 +911,7 @@
     def local_step(x_loc, wg, wu, wd, dy_loc):
         micro, rows, width = x_loc.shape
         wr, wc = wg.shape
+        fw = 2 * wc
         half = width // 2
         most = wr * 2 // 3
         tok = (micro, rows, width)
@@ -831,7 +919,7 @@
         n = 8 * micro * rows
 
         def ring_first(size):
-            return S((2, size // 2, 2 * wc), F32), S((2, 2, size // 2, 2 * wc), F32)
+            return S((2, size // 2, fw), F32), S((2, 2, size // 2, fw), F32)
 
         def pair_first(size):
             return S((4, size, wc), F32), S((2, size // 2, wc), F32)
@@ -845,10 +933,10 @@
             *pair_last(wr - most), *pair_last(wr),
         ]
         space = [
-            S((4, 2) + tok, BF16), S((4, 2) + tok, BF16), S((2 * wc, width), BF16),
-            S((2, 3) + tok_h, F32), S((4, 2) + tok_h, F32), S((4, 2) + tok_h, F32), S((3, 4, wr, 2 * wc), F32),
+            S((4, 2) + tok, BF16), S((4, 2) + tok, BF16), S((fw, width), BF16),
+            S((2, 3) + tok_h, F32), S((4, 2) + tok_h, F32), S((4, 2) + tok_h, F32), S((3, 4, wr, fw), F32),
             S((2, 2) + tok_h[1:], F32), S((2, 2) + tok_h[1:], F32), S((2, 2, 2) + tok_h[1:], F32),
-            S((4,) + tok_h, F32), S((2,) + tok_h[1:], F32), S((3, 4, wr, 2 * wc), F32),
+            S((4,) + tok_h, F32), S((2,) + tok_h[1:], F32), S((3, 4, wr, fw), F32),
             *ring_first(wr), *ring_first(most), *pair_first(wr - most), *pair_first(wr),
         ]
         res = pl.pallas_call(
@@ -858,25 +946,19 @@
             in_specs=[hbm] * 5,
             out_specs=[hbm] * (len(outs) + len(space)),
             scratch_shapes=[
-                V((width, 2 * wc), BF16), V((width, 2 * wc), BF16), V((2 * wc, width), BF16),
-                V((n, 2 * wc), BF16), V((n, 2 * wc), BF16), V((n, 2 * wc), BF16), V((n // 2, 2 * wc), BF16),
+                V((width, fw), BF16), V((width, fw), BF16), V((fw, width), BF16),
+                V((n, fw), BF16), V((n, fw), BF16), V((n, fw), BF16), V((n // 2, fw), BF16),
                 V((2, 2) + tok, BF16), V((2, 2) + tok, BF16),
                 V((2, 4, 2, micro, rows, wr), BF16), V((2, 4, 2, micro, rows, wr), BF16),
                 V((1, 2) + tok_h, F32), V((2, 2) + tok_h, F32),
-                V((2, 4, micro, rows, width // 4), F32), V((2, 2 * wc, width // 4), BF16), V((5, wr, 2 * wc), F32),
-                V((6, 2, rows, half), F32), V((6, wr // 2, 2 * wc), F32),
+                V((2, 4, micro, rows, width // 4), F32), V((2, fw, width // 4), BF16), V((6, wr, fw), F32),
+                V((5, 2, rows, half), F32), V((6, wr // 2, fw), F32),
                 dma((128,)), dma((200,)), dma((200,)),
             ],
             compiler_params=pltpu.CompilerParams(
                 collective_id=0, has_side_effects=True, vmem_limit_bytes=67_000_000
             ),
         )(x_loc, dy_loc, wg, wu, wd)
-        y_own, y_l2, r_own, r_lp, q_own, q_l2, g_own, g_lp, u_own, u_lp, v_own, v_l2, d_own, d_l2 = res[: len(outs)]
-        y_in = jnp.concatenate([y_l2[j, 0] + y_l2[j, 1] for j in range(2)], axis=2)
-        y = (x_loc.astype(F32) + (y_own + y_in)).astype(BF16)
-        dx = (dy_loc.astype(F32) + jnp.concatenate([r_own + r_lp, q_own + q_l2[0] + q_l2[1]], axis=2)).astype(BF16)
-        u_sum = jnp.concatenate([u_own + u_lp, v_own + (v_l2[0] + v_l2[1]).reshape(v_own.shape)], axis=0)
-        d_sum = d_own + (d_l2[0] + d_l2[1]).reshape(d_own.shape)
-        return y, dx, g_own + g_lp, u_sum, d_sum.T
+        return finish(x_loc, dy_loc, *res[: len(outs)])
 
     return jax.shard_map(local_step, mesh=mesh, in_specs=in_specs, out_specs=out_specs, check_vma=False)

time: 262 us -> 248 us (0.947)
  other arithmetic: 9.21 us -> 0 us
  local copies, waits for them, and re-layouts: 7.52 us -> 0 us
    pallas_call x0 -> x1, Pallas kernels: none -> 8.13 us  [finish(): pl.pallas_call(finish_kernel, name='finish', grid=(n,), out_shape=(S(x.sh...]
    unnamed x33 -> x0, local copies, waits for them, and re-layouts: 7.52 us -> none
    add x9 -> x0, other arithmetic: 6.59 us -> none  [the longest x2 1.19 us: local_step(): d_sum = d_own + (d_l2[0] + d_l2[1]).reshape(d_own.shape)]
    pallas_call x1, Pallas kernels: 244 us -> 238 us  [local_step(): pl.pallas_call(layer_kernel, name='layer', out_shape=tuple(outs + space),...]
where the time goes in v3:
time: 248 us; the launch traced here: 247 us
  Pallas kernels  246 us (99%)
    pallas_call x1, Pallas kernels, local_step(): pl.pallas_call(layer_kernel, name='layer', out_shape=tuple(outs + space),...  238 us
    pallas_call x1, Pallas kernels, finish(): pl.pallas_call(finish_kernel, name='finish', grid=(n,), out_shape=(S(x.sh...  8.13 us

profile of v3, /device:TPU:1, one launch (start us, length us, event | category | flops | bytes accessed | tf_op | source)
XLA Modules:
  0.0 247.3 jit_solution(3348452792257778595)
XLA Ops:
  0.6 238.4 %layer.1 = (f32[2,64,3072]{2,1,0:T(8,128)}, f32[2,2,2,64,1536]{4,3,2,1,0:T(8,128)}, f32[2,64,1536]{2,1,0:T(8,128)}, f32[2,64,1536]{2,1,0:T(8,128)}, f32[2,64,153...) custom-call(bf16[2,64,3072]{2,1,0:T(8,128)(2,1)} %x_ref.3, ...), custom_call_target="tpu_custom_call" | custom-call | tf_op jit(solution)/shard_map/layer/pallas_call | solution.py:942
  239.0 8.1 %finish.1 = (bf16[2,64,3072]{2,1,0:T(8,128)(2,1)}, bf16[2,64,3072]{2,1,0:T(8,128)(2,1)}, f32[384,512]{1,0:T(8,128)}, f32[384,512]{1,0:T(8,128)}, f32[512,384]{1,0:T(8,128)}) custom-call(bf16[2,64,3072]{2,1,0:T(8,128)(2,1)} %x_ref.3, bf16[2,64,3072]{2,1,0:T(8,128)(2,1)} %dy_ref.3, f32[2,64,3072]{2,1,0:T(8,128)} %get-tuple-element.19.y_own, ...), custom_call_target="tpu_custom_call" | custom-call | tf_op jit(solution)/shard_map/finish/pallas_call | solution.py:885

commit v4 on v3

--- a/solution.py
+++ b/solution.py
@@ -14,19 +14,20 @@
 ICI_RATE = 45.0e3
 CORE_RATE = 550.0e3
 HBM_RATE = 2.5e6
-MARGIN = 0.5
+MARGIN = 0.3
 FIRST, NEXT, EARLY = 0.5, 1, 0.01
 SIDES = (0, 1)
+TW, TR, TK, WK = 6, 3, 4, 6
 RING = 4
 AROUND = (1, 3, 2)
 BLOCKS = {
     "A": (("o", 0), ("o", 1)), "B": (("-", 0), ("+", 0)), "C": (("-", 1), ("+", 1)), "D": (("2", 0),), "E": (("2", 1),),
 }
 STEPS = (
-    "HAa", "HBa", "HBb", "HAb", "HDb", "HCb", "HCa", "HDa", "HEb", "HEa",
-    "R2", "W0au", "W0ad", "W0bu", "W0bd", "R+", "W0bg", "W0ag", "W2a", "R-",
-    "Q+", "Q2", "W2b", "W1a", "W3b", "Y2", "W1b", "Y0", "Y1", "Qo",
-    "Q-", "Ro", "W3a", "Y3",
+    "HBa", "HAa", "HBb", "HAb", "HDb", "HCb", "HDa", "HCa", "HEb", "HEa",
+    "W0au", "W0ad", "W0bu", "R2", "W0bd", "R+", "W0ag", "W0bg", "W1a", "Q+",
+    "R-", "Y1", "W1b", "W2a", "Q2", "Y0", "Q-", "W2b", "Ro", "Y2",
+    "Qo", "Y3", "W3b", "W3a",
 )
 
 
@@ -368,16 +369,16 @@
     for h, link in enumerate(links):
         go("2", h, [], [], link, l1.at[h], come[h])
     for k, (link, name) in enumerate(zip(links, "+-")):
-        go(name, 1 - k, [], [], link, l2.at[k, 1 - k], near[1 - k])
-        go(name, k, [l1.at[k]], [come[k]], link, l2.at[k, k], near[k])
+        go(name, 1 - k, [], [], link, l2(k, 1 - k), near[1 - k][1])
+        go(name, k, [l1.at[k]], [come[k]], link, l2(k, k), near[k][0])
 
 
 def layer_kernel(
     x_ref, dy_ref, wg_ref, wu_ref, wd_ref,
-    y_own, y_l2, r_own, r_lp, q_own, q_l2, g_own, g_lp, u_own, u_lp, v_own, v_l2, d_own, d_l2,
-    x_all, dy_all, wd_ext, y_pt, r_pt, q_pt, w_pt, y_l1, r_l1, r_l2, q_lp, q_l1, w_lc,
-    g_l1, g_l2, u_l1, u_l2, v_lp, v_l1, d_lp, d_l1,
-    wg_all, wu_all, wd_all, h_all, da_all, db_all, h_ext, xb, db, xs, ds, r_out, q_out, y_out, wx, tw, tk, wk,
+    y_own, y_late, r_own, r_lp, q_own, q_late, g_own, g_lp, u_own, u_lp, v_own, v_late, d_own, d_late,
+    x_all, dy_all, wd_ext, y_pt, y_mine, r_pt, q_pt, w_pt, y_l1, y_soon, r_l1, r_l2, q_lp, q_l1, q_soon, w_lc,
+    g_l1, g_l2, u_l1, u_l2, v_lp, v_l1, v_soon, d_lp, d_l1, d_soon,
+    wg_all, wu_all, wd_all, h_all, da_all, db_all, h_ext, xb, db, xs, ds, r_out, q_out, y_out, wx, tw, tr, tk, wk,
     local_sems, send_sems, recv_sems,
 ):
     here = Place()
@@ -387,7 +388,8 @@
     x, xp, xm, x2, a, c = here.x, here.xp, here.xm, here.x2, here.a, here.c
     micro, rows, width = x_ref.shape
     wr, wc = wg_ref.shape
-    half_width = width // 2
+    r_cols = width // 3
+    q_cols = width - r_cols
     edge = width * 5 // 24
     m_blk = micro * rows
     n_blk = 2 * m_blk
@@ -496,7 +498,8 @@
     y_pool = Pool([y_out.at[i] for i in range(y_out.shape[0])])
     ext_pool = Pool([wx.at[i] for i in range(wx.shape[0])])
     wout_pool = Pool([tw.at[i] for i in range(tw.shape[0])])
-    tk_pool = Pool([tk.at[i] for i in range(tk.shape[0])])
+    pair_pool = Pool([tr.at[i] for i in range(tr.shape[0])])
+    row_pool = Pool([tk.at[i] for i in range(tk.shape[0])])
     wk_pool = Pool([wk.at[i] for i in range(wk.shape[0])])
 
     first_slot = tok_pool.take(1)[0]
@@ -567,7 +570,7 @@
                 hidden[piece].hit()
 
         net.job([tokens_in[piece] for piece in block], [(tok_pool, 1)], load, rank * EARLY, "load")
-        net.job([loaded, weights_in[turn]], [], multiply, rank, "mxu", 1.2 + 0.8 * count)
+        net.job([loaded, weights_in[turn]], [], multiply, rank, "mxu", 1.3 + 0.85 * count)
 
     def give_hidden(name):
         def go():
@@ -583,16 +586,16 @@
 
     r_in = {k: Flag() for k in zs}
     q_in = {k: Flag() for k in zs}
-    tile_dx = half_width // 2
-
-    def rows_of(name, pool, part, flag, col0, rank):
+    tile_dx = r_cols
+
+    def rows_of(name, pool, part, flag, col0, cols, rank):
         at = rows_at(zs[name] * n_blk, n_blk)
 
         def multiply(slots):
             i = slots[0]
             ref = pool.refs[i]
 
-            @pl.loop(0, half_width // tile_dx)
+            @pl.loop(0, cols // tile_dx)
             def _(j):
                 src = rows_at(col0 + j * tile_dx, tile_dx)
                 val = dot(da_all[at, :], wg_all[src, :], 1, 1) + dot(db_all[at, :], wu_all[src, :], 1, 1)
@@ -602,11 +605,11 @@
             pool.give(i, [done])
             net.when([done], flag.hit)
 
-        net.job([hidden[name, side] for side in SIDES], [(pool, 1)], multiply, rank, "mxu", 2.0)
+        net.job([hidden[name, side] for side in SIDES], [(pool, 1)], multiply, rank, "mxu", 1.4 * cols // tile_dx)
 
     for name in zs:
-        rows_of(name, r_pool, r_pt, r_in[name], 0, ranks["R" + name])
-        rows_of(name, q_pool, q_pt, q_in[name], half_width, ranks["Q" + name])
+        rows_of(name, r_pool, r_pt, r_in[name], 0, r_cols, ranks["R" + name])
+        rows_of(name, q_pool, q_pt, q_in[name], r_cols, q_cols, ranks["Q" + name])
 
     quarter = width // 4
     tile_y = quarter // 3 if quarter % 3 == 0 else quarter
@@ -639,27 +642,25 @@
             ext_pool.give(held[0])
             half = pl.ds((j % 2) * quarter, quarter)
             out = [net.copy(ref.at[k], y_pt.at[j // 2, k, :, :, half]) for k in range(3)]
-            out.append(net.copy(ref.at[3], y_own.at[:, :, cols]))
+            out.append(net.copy(ref.at[3], y_mine.at[j // 2, :, :, half]))
             y_pool.give(i, out)
             net.when(out, y_in[j // 2].hit)
 
         net.job([ext_in], [(ext_pool, 1)], load, ranks["Y%d" % j] * EARLY, "ext")
         own = [hidden[name, 0] for name in zs]
-        net.job([loaded, ext_rows] + own, [(y_pool, 1)], multiply, ranks["Y%d" % j], "mxu", 2.1)
+        net.job([loaded, ext_rows] + own, [(y_pool, 1)], multiply, ranks["Y%d" % j], "mxu", 2.3)
 
     for j in range(4):
         y_of(j)
 
-    def tok_view(ref, shape):
-        return ref if len(shape) == 3 else ref.at[0]
-
-    tok_add = Adder(net, tk_pool, tok_view)
+    pair_add = Adder(net, pair_pool, lambda ref, shape: ref)
+    row_add = Adder(net, row_pool, lambda ref, shape: ref.at[:, pl.ds(0, shape[-1])])
     names = {name: k for k, name in enumerate(ORDER)}
 
-    r_near = [Flag(2), Flag(2)]
+    r_near = [[Flag(), Flag()] for _ in SIDES]
     ring_reduce(
-        net, tok_add, lambda name, h: [r_in[name]], lambda name, h: [r_pt.at[zs[name], :, h]],
-        r_l1, r_l2, ring_z, r_near,
+        net, pair_add, lambda name, h: [r_in[name]], lambda name, h: [r_pt.at[zs[name], :, h]],
+        r_l1, lambda k, h: r_l2.at[k, h], ring_z, r_near,
     )
 
     def r_last(h):
@@ -669,8 +670,8 @@
             got, _ = net.send("tok", away, r_lp.at[h])
             net.when([got], nothing)
 
-        tok_add.add(
-            [r_in["o"], r_near[h]], [r_pt.at[z, :, h], r_l2.at[0, h], r_l2.at[1, h]],
+        pair_add.add(
+            [r_in["o"], *r_near[h]], [r_pt.at[z, :, h], r_l2.at[0, h], r_l2.at[1, h]],
             lambda ref: [(ref.at[1 - b], away), (ref.at[b], r_own.at[h])], go,
         )
 
@@ -678,10 +679,16 @@
     r_last(1)
 
     for j in range(2):
+        y_near = [[Flag(), Flag()] for _ in SIDES]
         ring_reduce(
-            net, tok_add, lambda name, h, j=j: [y_in[j]], lambda name, h, j=j: [y_pt.at[j, names[name], h]],
-            y_l1.at[j], y_l2.at[j], ring_z, [Flag(2), Flag(2)],
+            net, row_add, lambda name, h, j=j: [y_in[j]], lambda name, h, j=j: [y_pt.at[j, names[name], h]],
+            y_l1.at[j], lambda k, h, j=j: (y_late if k == h else y_soon).at[j, h], ring_z, y_near,
         )
+        for h in SIDES:
+            row_add.add(
+                [y_in[j], y_near[h][1]], [y_mine.at[j, h], y_soon.at[j, h]],
+                lambda ref, j=j, h=h: [(ref, y_own.at[j, h])], nothing,
+            )
 
     q_pair = {k: Flag() for k in zs}
 
@@ -693,13 +700,17 @@
 
     for name in ORDER:
         pair_q(name)
+    q_near = [[Flag(), Flag()] for _ in SIDES]
     ring_reduce(
-        net, tok_add, lambda name, h: [q_in[name], q_pair[name]],
-        lambda name, h: [q_pt.at[zs[name], b, h], q_lp.at[names[name], h]], q_l1, q_l2, ring_z, [Flag(2), Flag(2)],
+        net, row_add, lambda name, h: [q_in[name], q_pair[name]],
+        lambda name, h: [q_pt.at[zs[name], b, h], q_lp.at[names[name], h]],
+        q_l1, lambda k, h: (q_late if k == h else q_soon).at[h], ring_z, q_near,
     )
-    tok_add.add(
-        [q_in["o"], q_pair["o"]], [q_pt.at[z, b], q_lp.at[3]], lambda ref: [(ref, q_own)], nothing,
-    )
+    for h in SIDES:
+        row_add.add(
+            [q_in["o"], q_pair["o"], q_near[h][1]], [q_pt.at[z, b, h], q_lp.at[3, h], q_soon.at[h]],
+            lambda ref, h=h: [(ref, q_own.at[h])], nothing,
+        )
 
     tile_w = wc
     n_tok = 4 * n_blk
@@ -768,9 +779,9 @@
         if k == 0:
             last = max(mats, key=lambda m: ranks[step + "gud"[m]])
             for m in range(3):
-                net.job(flags, [(wout_pool, 1)], multiply([m], m == last), ranks[step + "gud"[m]], "mxu", 1.15)
+                net.job(flags, [(wout_pool, 1)], multiply([m], m == last), ranks[step + "gud"[m]], "mxu", 1.25)
         else:
-            net.job(flags, [(wout_pool, len(mats))], multiply(mats, True), ranks[step], "mxu", 2.8)
+            net.job(flags, [(wout_pool, len(mats))], multiply(mats, True), ranks[step], "mxu", 3.0)
 
     for k, name in enumerate(ORDER):
         grads_of(k, name, 1 - c, 0)
@@ -786,10 +797,10 @@
         def part(ref, h):
             return ref.at[pl.ds(row0 + h * (size // 2), size // 2)]
 
-        near = [Flag(2), Flag(2)]
+        near = [[Flag(), Flag()] for _ in SIDES]
         ring_reduce(
             net, w_add, lambda name, h: [w_in[m, names[name]]],
-            lambda name, h: [part(w_pt.at[m, names[name]], h)], l1, l2, ring_x, near,
+            lambda name, h: [part(w_pt.at[m, names[name]], h)], l1, lambda k, h: l2.at[k, h], ring_x, near,
         )
 
         def last(h):
@@ -801,14 +812,14 @@
                 net.when([got], nothing)
 
             w_add.add(
-                [w_in[m, 3], near[h]], [block, l2.at[0, h], l2.at[1, h]],
+                [w_in[m, 3], *near[h]], [block, l2.at[0, h], l2.at[1, h]],
                 lambda ref: [(ref.at[:, other], away), (ref.at[:, mine], row_half(own, h))], go,
             )
 
         last(0)
         last(1)
 
-    def w_pair_first(m, row0, size, lp, l1, l2, own):
+    def w_pair_first(m, row0, size, lp, l1, soon, late, own):
         def part(ref, h):
             return ref.at[pl.ds(row0 + h * (size // 2), size // 2)]
 
@@ -833,70 +844,72 @@
         def ready(name, h):
             return have[names[name]] + [pair[names[name], h]]
 
-        ring_reduce(net, w_add, ready, terms, l1, l2, ring_x, [Flag(2), Flag(2)])
-        for h in range(2):
-            w_add.add(ready("o", h), terms("o", h), lambda ref, h=h: [(ref, row_half(own, h))], nothing)
+        near = [[Flag(), Flag()] for _ in SIDES]
+        ring_reduce(
+            net, w_add, ready, terms, l1, lambda k, h: row_half(late if k == h else soon, h), ring_x, near,
+        )
+        for h in SIDES:
+            w_add.add(
+                ready("o", h) + [near[h][1]], terms("o", h) + [row_half(soon, h)],
+                lambda ref, h=h: [(ref, row_half(own, h))], nothing,
+            )
 
     most = wr * 2 // 3
     w_ring_first(0, 0, wr, g_l1, g_l2, g_lp, g_own)
-    w_pair_first(2, 0, wr, d_lp, d_l1, d_l2, d_own)
+    w_pair_first(2, 0, wr, d_lp, d_l1, d_soon, d_late, d_own)
     w_ring_first(1, 0, most, u_l1, u_l2, u_lp, u_own)
-    w_pair_first(1, most, wr - most, v_lp, v_l1, v_l2, v_own)
+    w_pair_first(1, most, wr - most, v_lp, v_l1, v_soon, v_late, v_own)
     net.run()
 
 
 def finish_kernel(
-    x_ref, dy_ref, y_own, y_l2, r_own, r_lp, q_own, q_l2, g_own, g_lp, u_own, u_lp, v_own, v_l2, d_own, d_l2,
+    x_ref, dy_ref, y_own, y_late, r_own, r_lp, q_own, q_late, g_own, g_lp, u_own, u_lp, v_own, v_late, d_own, d_late,
     y_ref, dx_ref, g_ref, u_ref, d_ref,
 ):
-    i = pl.program_id(0)
-    half = r_own.shape[-1]
+    half, low = y_own.shape[-1], r_own.shape[-1]
     for j in range(2):
         cols = pl.ds(j * half, half)
-        total = y_own[:, :, cols] + y_l2[j, 0] + y_l2[j, 1]
-        y_ref[:, :, cols] = (x_ref[:, :, cols].astype(F32) + total).astype(BF16)
-    low, high = pl.ds(0, half), pl.ds(half, half)
-    dx_ref[:, :, low] = (dy_ref[:, :, low].astype(F32) + (r_own[...] + r_lp[...])).astype(BF16)
-    dx_ref[:, :, high] = (dy_ref[:, :, high].astype(F32) + (q_own[...] + q_l2[0] + q_l2[1])).astype(BF16)
+        y_ref[:, :, cols] = (x_ref[:, :, cols].astype(F32) + (y_own[j] + y_late[j])).astype(BF16)
+    for cols, own, late in ((pl.ds(0, low), r_own, r_lp), (pl.ds(low, q_own.shape[-1]), q_own, q_late)):
+        dx_ref[:, :, cols] = (dy_ref[:, :, cols].astype(F32) + (own[...] + late[...])).astype(BF16)
     g_ref[...] = g_own[...] + g_lp[...]
-    most, size, rest = u_own.shape[0] * pl.num_programs(0), u_own.shape[0], v_own.shape[0]
-    u_ref[pl.ds(pl.multiple_of(i * size, size), size), :] = u_own[...] + u_lp[...]
-    u_ref[pl.ds(pl.multiple_of(4 * size + i * rest, rest), rest), :] = v_own[...] + v_l2[0, 0] + v_l2[1, 0]
-    rows, cols = d_own.shape
-    total = d_own[...] + d_l2[0].reshape(rows, cols) + d_l2[1].reshape(rows, cols)
-    d_ref[...] = total.T
-
-
-def finish(x, dy, y_own, y_l2, r_own, r_lp, q_own, q_l2, g_own, g_lp, u_own, u_lp, v_own, v_l2, d_own, d_l2):
+    row = 0
+    for own, late in ((u_own, u_lp), (v_own, v_late)):
+        size = own.shape[0]
+        at = pl.multiple_of(row + pl.program_id(0) * size, size)
+        u_ref[pl.ds(at, size), :] = own[...] + late[...]
+        row = size * pl.num_programs(0)
+    d_ref[...] = (d_own[...] + d_late[...]).T
+
+
+def finish(x, dy, y_own, y_late, *others):
     micro, rows, width = x.shape
+    r_own, g_own = others[0], others[4]
     wr, wc = g_own.shape
-    half = width // 2
     n = 4
-    B = pl.BlockSpec
     S = jax.ShapeDtypeStruct
 
-    def tok(cols):
-        return B((micro, rows // n, cols), lambda i: (0, i, 0))
-
-    def flat(rows, cols):
-        return B((rows // n, cols), lambda i: (i, 0))
-
-    most, rest = u_own.shape[0], v_own.shape[0]
+    def tok(array):
+        return pl.BlockSpec((micro, rows // n, array.shape[-1]), lambda i: (0, i, 0))
+
+    def flat(array):
+        return pl.BlockSpec((array.shape[0] // n, wc), lambda i: (i, 0))
+
+    halves = pl.BlockSpec((2, micro, rows // n, width // 2), lambda i: (0, 0, i, 0))
+    turned = pl.BlockSpec((wr, wc // n), lambda i: (0, i))
     return pl.pallas_call(
         finish_kernel,
         name="finish",
         grid=(n,),
         out_shape=(S(x.shape, BF16), S(x.shape, BF16), S((wr, wc), F32), S((wr, wc), F32), S((wc, wr), F32)),
         in_specs=[
-            tok(width), tok(width), tok(width), B((2, 2, micro, rows // n, half), lambda i: (0, 0, 0, i, 0)),
-            tok(half), tok(half), tok(half), B((2, micro, rows // n, half), lambda i: (0, 0, i, 0)),
-            flat(wr, wc), flat(wr, wc), flat(most, wc), flat(most, wc),
-            flat(rest, wc), B((2, 1, rest // n, wc), lambda i: (0, i // 2, i % 2, 0)),
-            B((wr, wc // n), lambda i: (0, i)), B((2, 2, wr // 2, wc // n), lambda i: (0, 0, 0, i)),
+            tok(x), tok(x), halves, halves, *map(tok, others[:4]), *map(flat, others[4:10]), turned, turned,
         ],
-        out_specs=[tok(width), tok(width), flat(wr, wc), B((wr, wc), lambda i: (0, 0)), B((wc // n, wr), lambda i: (i, 0))],
+        out_specs=[
+            tok(x), tok(x), flat(g_own), pl.BlockSpec((wr, wc), lambda i: (0, 0)), pl.BlockSpec((wc // n, wr), lambda i: (i, 0)),
+        ],
         compiler_params=pltpu.CompilerParams(vmem_limit_bytes=60 * 2**20),
-    )(x, dy, y_own, y_l2, r_own, r_lp, q_own, q_l2, g_own, g_lp, u_own, u_lp, v_own, v_l2, d_own, d_l2)
+    )(x, dy, y_own, y_late, *others)
 
 
 def solution(mesh):
@@ -912,33 +925,32 @@
         micro, rows, width = x_loc.shape
         wr, wc = wg.shape
         fw = 2 * wc
-        half = width // 2
         most = wr * 2 // 3
+        few = wr - most
+        r_cols = width // 3
+        n = 8 * micro * rows
         tok = (micro, rows, width)
-        tok_h = (micro, rows, half)
-        n = 8 * micro * rows
-
-        def ring_first(size):
-            return S((2, size // 2, fw), F32), S((2, 2, size // 2, fw), F32)
-
-        def pair_first(size):
-            return S((4, size, wc), F32), S((2, size // 2, wc), F32)
-
-        def pair_last(size):
-            return S((size, wc), F32), S((2, 2, size // 2, wc), F32)
+        half, tok_r, tok_q = ((micro, rows, w) for w in (width // 2, r_cols, width - r_cols))
+        two = (2,)
+
+        def f32(*shape):
+            return S(shape, F32)
 
         outs = [
-            S(tok, F32), S((2, 2) + tok_h, F32), S(tok_h, F32), S(tok_h, F32), S(tok_h, F32), S((2,) + tok_h, F32),
-            S((wr, wc), F32), S((wr, wc), F32), S((most, wc), F32), S((most, wc), F32),
-            *pair_last(wr - most), *pair_last(wr),
+            f32(*two, *half), f32(*two, *half), f32(*tok_r), f32(*tok_r), f32(*tok_q), f32(*tok_q),
+            *[f32(size, wc) for size in (wr, wr, most, most, few, few, wr, wr)],
         ]
+        weights = f32(3, 4, wr, fw)
         space = [
             S((4, 2) + tok, BF16), S((4, 2) + tok, BF16), S((fw, width), BF16),
-            S((2, 3) + tok_h, F32), S((4, 2) + tok_h, F32), S((4, 2) + tok_h, F32), S((3, 4, wr, fw), F32),
-            S((2, 2) + tok_h[1:], F32), S((2, 2) + tok_h[1:], F32), S((2, 2, 2) + tok_h[1:], F32),
-            S((4,) + tok_h, F32), S((2,) + tok_h[1:], F32), S((3, 4, wr, fw), F32),
-            *ring_first(wr), *ring_first(most), *pair_first(wr - most), *pair_first(wr),
+            f32(2, 3, *half), f32(*two, *half), f32(4, 2, *tok_r), f32(4, 2, *tok_q), weights,
+            f32(*two, *half), f32(*two, *half), f32(*two, *tok_r), f32(*two, *two, *tok_r),
+            f32(4, *tok_q), f32(*tok_q), f32(*tok_q), weights,
         ]
+        for size in (wr // 2, most // 2):
+            space += [f32(*two, size, fw), f32(*two, *two, size, fw)]
+        for size in (few, wr):
+            space += [f32(4, size, wc), f32(*two, size // 2, wc), f32(size, wc)]
         res = pl.pallas_call(
             layer_kernel,
             name="layer",
@@ -950,9 +962,9 @@
                 V((n, fw), BF16), V((n, fw), BF16), V((n, fw), BF16), V((n // 2, fw), BF16),
                 V((2, 2) + tok, BF16), V((2, 2) + tok, BF16),
                 V((2, 4, 2, micro, rows, wr), BF16), V((2, 4, 2, micro, rows, wr), BF16),
-                V((1, 2) + tok_h, F32), V((2, 2) + tok_h, F32),
-                V((2, 4, micro, rows, width // 4), F32), V((2, fw, width // 4), BF16), V((6, wr, fw), F32),
-                V((5, 2, rows, half), F32), V((6, wr // 2, fw), F32),
+                V((1, 2) + tok_r, F32), V((2, 2) + tok_q, F32),
+                V((2, 4, micro, rows, width // 4), F32), V((2, fw, width // 4), BF16), V((TW, wr, fw), F32),
+                V((TR,) + tok_r, F32), V((TK,) + tok_q[1:], F32), V((WK, wr // 2, fw), F32),
                 dma((128,)), dma((200,)), dma((200,)),
             ],
             compiler_params=pltpu.CompilerParams(

time: 248 us -> 244 us (0.984)
  Pallas kernels: 246 us -> 242 us
    pallas_call x1, Pallas kernels: 238 us -> 235 us  [local_step(): pl.pallas_call(layer_kernel, name='layer', out_shape=tuple(outs + space),...]
where the time goes in v4:
time: 244 us; the launch traced here: 243 us
  Pallas kernels  242 us (99%)
    pallas_call x1, Pallas kernels, local_step(): pl.pallas_call(layer_kernel, name='layer', out_shape=tuple(outs + space),...  235 us
    pallas_call x1, Pallas kernels, finish(): pl.pallas_call(finish_kernel, name='finish', grid=(n,), out_shape=(S(x.sh...  7.23 us

profile of v4, /device:TPU:1, one launch (start us, length us, event | category | flops | bytes accessed | tf_op | source)
XLA Modules:
  0.0 243.2 jit_solution(5182971296705501421)
XLA Ops:
  0.6 235.1 %layer.1 = (f32[2,2,64,1536]{3,2,1,0:T(8,128)}, f32[2,2,64,1536]{3,2,1,0:T(8,128)}, f32[2,64,1024]{2,1,0:T(8,128)}, f32[2,64,1024]{2,1,0:T(8,128)}, f32[2,64,204...) custom-call(bf16[2,64,3072]{2,1,0:T(8,128)(2,1)} %x_ref.3, ...), custom_call_target="tpu_custom_call" | custom-call | tf_op jit(solution)/shard_map/layer/pallas_call | solution.py:954
  235.8 7.2 %finish.1 = (bf16[2,64,3072]{2,1,0:T(8,128)(2,1)}, bf16[2,64,3072]{2,1,0:T(8,128)(2,1)}, f32[384,512]{1,0:T(8,128)}, f32[384,512]{1,0:T(8,128)}, f32[512,384]{1,0:T(8,128)}) custom-call(bf16[2,64,3072]{2,1,0:T(8,128)(2,1)} %x_ref.3, bf16[2,64,3072]{2,1,0:T(8,128)(2,1)} %dy_ref.3, f32[2,2,64,1536]{3,2,1,0:T(8,128)} %get-tuple-element.19.y_own, ...), custom_call_target="tpu_custom_call" | custom-call | tf_op jit(solution)/shard_map/finish/pallas_call | solution.py:900

commit v5 on v4

--- a/solution.py
+++ b/solution.py
@@ -17,17 +17,18 @@
 MARGIN = 0.3
 FIRST, NEXT, EARLY = 0.5, 1, 0.01
 SIDES = (0, 1)
-TW, TR, TK, WK = 6, 3, 4, 6
+TW, TR, TK, WK = 6, 3, 4, 5
+COPIES = 224
 RING = 4
 AROUND = (1, 3, 2)
 BLOCKS = {
     "A": (("o", 0), ("o", 1)), "B": (("-", 0), ("+", 0)), "C": (("-", 1), ("+", 1)), "D": (("2", 0),), "E": (("2", 1),),
 }
 STEPS = (
-    "HBa", "HAa", "HBb", "HAb", "HDb", "HCb", "HDa", "HCa", "HEb", "HEa",
-    "W0au", "W0ad", "W0bu", "R2", "W0bd", "R+", "W0ag", "W0bg", "W1a", "Q+",
-    "R-", "Y1", "W1b", "W2a", "Q2", "Y0", "Q-", "W2b", "Ro", "Y2",
-    "Qo", "Y3", "W3b", "W3a",
+    "HBa", "HAa", "HBb", "HAb", "HDb", "HCb", "HDa", "HCa", "R+", "HEb",
+    "W0ag1", "W0au1", "HEa", "W0bu1", "W0bg1", "R2", "W0ad1", "W0ad0", "W0ag0", "W0bd1",
+    "W0au0", "W0bg0", "R-", "W2a", "W0bd0", "W0bu0", "Q+", "Ro", "W2b", "Y3",
+    "Q2", "Y2", "W1a", "W1b", "W3a", "Y0", "Y1", "Q-", "Qo", "W3b",
 )
 
 
@@ -150,7 +151,7 @@
         self.free[link] = end
         sent = Handle(end + 0.5, copy.wait_send)
         self.open.append(sent)
-        return Handle(end + 2.0, arrive.wait_recv), sent
+        return Handle(end + (1.0 if link == "core" else 2.0), arrive.wait_recv), sent
 
     def copy(self, src, dst):
         if self.local_free:
@@ -368,7 +369,8 @@
 
     for h, link in enumerate(links):
         go("2", h, [], [], link, l1.at[h], come[h])
-    for k, (link, name) in enumerate(zip(links, "+-")):
+    for k, link in enumerate(links):
+        name = link[-1]
         go(name, 1 - k, [], [], link, l2(k, 1 - k), near[1 - k][1])
         go(name, k, [l1.at[k]], [come[k]], link, l2(k, k), near[k][0])
 
@@ -516,7 +518,7 @@
 
     ranks = {step: 10 + i for i, step in enumerate(STEPS)}
 
-    hidden = {piece: Flag(2) for piece in pieces}
+    hidden = {(piece, turn): Flag() for piece in pieces for turn in SIDES}
     ext_rows = Flag(4)
     tile_h = min(256, wc)
 
@@ -567,16 +569,19 @@
 
             tok_pool.give(i)
             for piece in block:
-                hidden[piece].hit()
+                hidden[piece, turn].hit()
 
         net.job([tokens_in[piece] for piece in block], [(tok_pool, 1)], load, rank * EARLY, "load")
         net.job([loaded, weights_in[turn]], [], multiply, rank, "mxu", 1.3 + 0.85 * count)
+
+    def both(piece):
+        return [hidden[piece, turn] for turn in SIDES]
 
     def give_hidden(name):
         def go():
             got, _ = net.send("tok", h_all.at[piece_rows((name, 1)), :], h_ext.at[rows_at(zs[name] * m_blk, m_blk), :])
             net.arrive(got, ext_rows)
-        net.job([hidden[name, 1]], [], go, NEXT)
+        net.job(both((name, 1)), [], go, NEXT)
 
     for key in BLOCKS:
         hidden_of(key, 0)
@@ -605,7 +610,7 @@
             pool.give(i, [done])
             net.when([done], flag.hit)
 
-        net.job([hidden[name, side] for side in SIDES], [(pool, 1)], multiply, rank, "mxu", 1.4 * cols // tile_dx)
+        net.job(both((name, 0)) + both((name, 1)), [(pool, 1)], multiply, rank, "mxu", 1.4 * cols // tile_dx)
 
     for name in zs:
         rows_of(name, r_pool, r_pt, r_in[name], 0, r_cols, ranks["R" + name])
@@ -647,7 +652,7 @@
             net.when(out, y_in[j // 2].hit)
 
         net.job([ext_in], [(ext_pool, 1)], load, ranks["Y%d" % j] * EARLY, "ext")
-        own = [hidden[name, 0] for name in zs]
+        own = [flag for name in zs for flag in both((name, 0))]
         net.job([loaded, ext_rows] + own, [(y_pool, 1)], multiply, ranks["Y%d" % j], "mxu", 2.3)
 
     for j in range(4):
@@ -712,17 +717,20 @@
             lambda ref, h=h: [(ref, q_own.at[h])], nothing,
         )
 
-    tile_w = wc
     n_tok = 4 * n_blk
-    w_in = {(m, k): Flag() for m in range(3) for k in range(4)}
-    w_side = {(m, k): Flag() for m in range(3) for k in range(4)}
-    all_hidden = list(hidden.values())
     mats = range(3)
+    keys = [(m, k, h) for m in mats for k in range(RING) for h in SIDES]
+    w_in = {key: Flag() for key in keys}
+    w_side = {key: Flag() for key in keys}
+    columns = (rows_at(a * wc, wc), rows_at((1 - a) * wc, wc))
 
     def grads_of(k, name, core, turn):
         loaded = Flag()
         held = []
         cols = rows_at((xs_of[name] * 2 + core) * wr, wr)
+        step = "W%d%s" % (k, "ab"[turn])
+        places = {}
+        uses = Flag(len(mats) * 2 if k == 0 else 1)
 
         def load(slots):
             i = slots[0]
@@ -730,58 +738,80 @@
             one, two = cut_pool.refs[i]
             net.when([net.copy(x_all.at[:, :, :, :, cols], one), net.copy(dy_all.at[:, :, :, :, cols], two)], loaded.hit)
 
-        def out(m, j, ref):
+        def out(m, h):
+            j, spent = places[m]
+            ref = wout_pool.refs[j].at[:, columns[h]]
+
+            def through(handle):
+                spent.append(handle)
+                if len(spent) == 2:
+                    wout_pool.give(j, spent)
+
             if turn == 0:
-                got, sent = net.send("core", ref, w_lc.at[m, k])
-                wout_pool.give(j, [sent])
-                net.arrive(got, w_side[m, k])
+                got, sent = net.send("core", ref, w_lc.at[m, k, :, columns[h]])
+                through(sent)
+                net.arrive(got, w_side[m, k, h])
                 return
 
             def begin(slots):
-                halves = [(nth(ref, h, 2), wk_pool.refs[i]) for h, i in enumerate(slots)]
-                loads = [net.copy(nth(w_lc.at[m, k], h, 2), slot) for h, (_, slot) in enumerate(halves)]
+                slot = wk_pool.refs[slots[0]]
 
                 def add():
-                    for i, (dst, slot) in zip(slots, halves):
-                        sum_rows(dst, [slot])
-                        wk_pool.give(i)
-                    net.now += 0.8
-                    done = net.copy(ref, w_pt.at[m, k])
-                    wout_pool.give(j, [done])
-                    net.when([done], w_in[m, k].hit)
-
-                net.when(loads, add)
-
-            net.job([w_side[m, k]], [(wk_pool, 2)], begin, FIRST)
-
-        def multiply(which, free):
-            def then(slots):
-                refs = [wout_pool.refs[j] for j in slots]
-                one, two = cut_pool.refs[held[0]]
-
-                @pl.loop(0, 2 * wc // tile_w)
-                def _(j):
-                    at = rows_at(j * tile_w, tile_w)
-                    for m, ref in zip(which, refs):
-                        cut = (two if m == 2 else one)[...].reshape(n_tok, wr)
-                        ref[:, at] = dot(cut, (da_all, db_all, h_all)[m][:, at], 0, 0)
-
-                if free:
-                    cut_pool.give(held[0])
-                for m, j, ref in zip(which, slots, refs):
-                    out(m, j, ref)
+                    sum_rows(ref, [slot])
+                    net.now += 0.4
+                    wk_pool.give(slots[0])
+                    done = net.copy(ref, w_pt.at[m, k, :, columns[h]])
+                    through(done)
+                    net.when([done], w_in[m, k, h].hit)
+
+                net.when([net.copy(w_lc.at[m, k, :, columns[h]], slot)], add)
+
+            net.job([w_side[m, k, h]], [(wk_pool, 1)], begin, FIRST)
+
+        def product(m, at):
+            one, two = cut_pool.refs[held[0]]
+            cut = (two if m == 2 else one)[...].reshape(n_tok, wr)
+            wout_pool.refs[places[m][0]][:, at] = dot(cut, (da_all, db_all, h_all)[m][:, at], 0, 0)
+
+        def used():
+            uses.hit()
+            if uses.left == 0:
+                cut_pool.give(held[0])
+
+        def some(m, h):
+            def then(*slots):
+                if slots:
+                    places[m] = (slots[0][0], [])
+                product(m, columns[h])
+                used()
+                out(m, h)
             return then
 
-        flags = [loaded] + all_hidden
-        step = "W%d%s" % (k, "ab"[turn])
-        first = min(ranks[step + m] for m in "gud") if k == 0 else ranks[step]
+        def all_of_it(slots):
+            for m in mats:
+                places[m] = (slots[m], [])
+
+            @pl.loop(0, 2)
+            def _(j):
+                for m in mats:
+                    product(m, rows_at(j * wc, wc))
+
+            used()
+            for h in SIDES:
+                for m in mats:
+                    out(m, h)
+
+        parts = [(m, h, ranks["%s%s%d" % (step, "gud"[m], h)]) for m in mats for h in SIDES] if k == 0 else []
+        first = min(rank for _, _, rank in parts) if parts else ranks[step]
         net.job(list(tokens_in.values()), [(cut_pool, 1)], load, first * EARLY, "cut")
-        if k == 0:
-            last = max(mats, key=lambda m: ranks[step + "gud"[m]])
-            for m in range(3):
-                net.job(flags, [(wout_pool, 1)], multiply([m], m == last), ranks[step + "gud"[m]], "mxu", 1.25)
-        else:
-            net.job(flags, [(wout_pool, len(mats))], multiply(mats, True), ranks[step], "mxu", 3.0)
+        own = [hidden[piece, 0] for piece in pieces]
+        other = [hidden[piece, 1] for piece in pieces]
+        for m, h, rank in parts:
+            begins = rank < ranks["%s%s%d" % (step, "gud"[m], 1 - h)]
+            needs = [(wout_pool, 1)] if begins else []
+            net.job([loaded] + (other if h else own), needs, some(m, h), rank, "mxu", 0.65)
+        if not parts:
+            net.job([loaded] + own + other, [(wout_pool, len(mats))], all_of_it, ranks[step], "mxu", 3.0)
 
     for k, name in enumerate(ORDER):
         grads_of(k, name, 1 - c, 0)
@@ -791,39 +821,32 @@
         return ref.at[pl.ds(0, shape[0]), pl.ds(0, shape[1])]
 
     w_add = Adder(net, wk_pool, w_view)
-    mine, other = rows_at(a * wc, wc), rows_at((1 - a) * wc, wc)
-
-    def w_ring_first(m, row0, size, l1, l2, lp, own):
-        def part(ref, h):
-            return ref.at[pl.ds(row0 + h * (size // 2), size // 2)]
+    mine, other = columns
+
+    def w_ring_first(m, row0, size, l1, l2, lp, own, links):
+        def part(k, h):
+            return w_pt.at[m, k, pl.ds(row0, size), columns[h]]
 
         near = [[Flag(), Flag()] for _ in SIDES]
         ring_reduce(
-            net, w_add, lambda name, h: [w_in[m, names[name]]],
-            lambda name, h: [part(w_pt.at[m, names[name]], h)], l1, lambda k, h: l2.at[k, h], ring_x, near,
+            net, w_add, lambda name, h: [w_in[m, names[name], h]], lambda name, h: [part(names[name], h)],
+            l1, lambda k, h: l2.at[k, h], links, near,
         )
 
-        def last(h):
-            block = part(w_pt.at[m, 3], h)
-            away = block.at[:, other]
-
-            def go():
-                got, _ = net.send("wgt", away, row_half(lp, h))
-                net.when([got], nothing)
-
-            w_add.add(
-                [w_in[m, 3], *near[h]], [block, l2.at[0, h], l2.at[1, h]],
-                lambda ref: [(ref.at[:, other], away), (ref.at[:, mine], row_half(own, h))], go,
-            )
-
-        last(0)
-        last(1)
+        def last(h, outs, then):
+            w_add.add([w_in[m, 3, h], *near[h]], [part(3, h), l2.at[0, h], l2.at[1, h]], outs, then)
+
+        def go():
+            got, _ = net.send("wgt", part(3, 1), lp)
+            net.when([got], nothing)
+
+        last(1, lambda ref: [(ref, part(3, 1))], go)
+        last(0, lambda ref: [(ref, own)], nothing)
 
     def w_pair_first(m, row0, size, lp, l1, soon, late, own):
         def part(ref, h):
             return ref.at[pl.ds(row0 + h * (size // 2), size // 2)]
 
-        have = {k: [w_in[m, k]] for k in range(4)}
         pair = {(k, h): Flag() for k in range(4) for h in range(2)}
 
         def away(k, h):
@@ -831,7 +854,7 @@
                 got, _ = net.send("wgt", part(w_pt.at[m, k], h).at[:, other], row_half(lp.at[k], h))
                 net.arrive(got, pair[k, h])
 
-            net.job(have[k], [], go, NEXT)
+            net.job([w_in[m, k, 1]], [], go, NEXT)
 
         for k in range(4):
             for h in range(2):
@@ -842,7 +865,7 @@
             return [part(w_pt.at[m, k], h).at[:, mine], row_half(lp.at[k], h)]
 
         def ready(name, h):
-            return have[names[name]] + [pair[names[name], h]]
+            return [w_in[m, names[name], 0], pair[names[name], h]]
 
         near = [[Flag(), Flag()] for _ in SIDES]
         ring_reduce(
@@ -855,9 +878,9 @@
             )
 
     most = wr * 2 // 3
-    w_ring_first(0, 0, wr, g_l1, g_l2, g_lp, g_own)
+    w_ring_first(0, 0, wr, g_l1, g_l2, g_lp, g_own, ring_x)
     w_pair_first(2, 0, wr, d_lp, d_l1, d_soon, d_late, d_own)
-    w_ring_first(1, 0, most, u_l1, u_l2, u_lp, u_own)
+    w_ring_first(1, 0, most, u_l1, u_l2, u_lp, u_own, ring_x[::-1])
     w_pair_first(1, most, wr - most, v_lp, v_l1, v_soon, v_late, v_own)
     net.run()
 
@@ -886,7 +909,7 @@
     micro, rows, width = x.shape
     r_own, g_own = others[0], others[4]
     wr, wc = g_own.shape
-    n = 4
+    n = 8
     S = jax.ShapeDtypeStruct
 
     def tok(array):
@@ -896,7 +919,8 @@
         return pl.BlockSpec((array.shape[0] // n, wc), lambda i: (i, 0))
 
     halves = pl.BlockSpec((2, micro, rows // n, width // 2), lambda i: (0, 0, i, 0))
-    turned = pl.BlockSpec((wr, wc // n), lambda i: (0, i))
+    lanes = wc // 4
+    turned = pl.BlockSpec((wr, lanes), lambda i: (0, i // 2))
     return pl.pallas_call(
         finish_kernel,
         name="finish",
@@ -906,7 +930,7 @@
             tok(x), tok(x), halves, halves, *map(tok, others[:4]), *map(flat, others[4:10]), turned, turned,
         ],
         out_specs=[
-            tok(x), tok(x), flat(g_own), pl.BlockSpec((wr, wc), lambda i: (0, 0)), pl.BlockSpec((wc // n, wr), lambda i: (i, 0)),
+            tok(x), tok(x), flat(g_own), pl.BlockSpec((wr, wc), lambda i: (0, 0)), pl.BlockSpec((lanes, wr), lambda i: (i // 2, 0)),
         ],
         compiler_params=pltpu.CompilerParams(vmem_limit_bytes=60 * 2**20),
     )(x, dy, y_own, y_late, *others)
@@ -947,8 +971,8 @@
             f32(*two, *half), f32(*two, *half), f32(*two, *tok_r), f32(*two, *two, *tok_r),
             f32(4, *tok_q), f32(*tok_q), f32(*tok_q), weights,
         ]
-        for size in (wr // 2, most // 2):
-            space += [f32(*two, size, fw), f32(*two, *two, size, fw)]
+        for size in (wr, most):
+            space += [f32(*two, size, wc), f32(*two, *two, size, wc)]
         for size in (few, wr):
             space += [f32(4, size, wc), f32(*two, size // 2, wc), f32(size, wc)]
         res = pl.pallas_call(
@@ -964,8 +988,8 @@
                 V((2, 4, 2, micro, rows, wr), BF16), V((2, 4, 2, micro, rows, wr), BF16),
                 V((1, 2) + tok_r, F32), V((2, 2) + tok_q, F32),
                 V((2, 4, micro, rows, width // 4), F32), V((2, fw, width // 4), BF16), V((TW, wr, fw), F32),
-                V((TR,) + tok_r, F32), V((TK,) + tok_q[1:], F32), V((WK, wr // 2, fw), F32),
-                dma((128,)), dma((200,)), dma((200,)),
+                V((TR,) + tok_r, F32), V((TK,) + tok_q[1:], F32), V((WK, wr, wc), F32),
+                dma((64,)), dma((COPIES,)), dma((COPIES,)),
             ],
             compiler_params=pltpu.CompilerParams(
                 collective_id=0, has_side_effects=True, vmem_limit_bytes=67_000_000

time: 244 us -> 243 us (level)
    pallas_call x1, Pallas kernels: 235 us -> 232 us  [local_step(): pl.pallas_call(layer_kernel, name='layer', out_shape=tuple(outs + space),...]
where the time goes in v5:
time: 243 us; the launch traced here: 242 us
  Pallas kernels  241 us (99%)
    pallas_call x1, Pallas kernels, local_step(): pl.pallas_call(layer_kernel, name='layer', out_shape=tuple(outs + space),...  232 us
    pallas_call x1, Pallas kernels, finish(): pl.pallas_call(finish_kernel, name='finish', grid=(n,), out_shape=(S(x.sh...  8.7 us

profile of v5, /device:TPU:1, one launch (start us, length us, event | category | flops | bytes accessed | tf_op | source)
XLA Modules:
  0.0 241.9 jit_solution(1613403571794890922)
XLA Ops:
  0.6 232.4 %layer.1 = (f32[2,2,64,1536]{3,2,1,0:T(8,128)}, f32[2,2,64,1536]{3,2,1,0:T(8,128)}, f32[2,64,1024]{2,1,0:T(8,128)}, f32[2,64,1024]{2,1,0:T(8,128)}, f32[2,64,204...) custom-call(bf16[2,64,3072]{2,1,0:T(8,128)(2,1)} %x_ref.3, ...), custom_call_target="tpu_custom_call" | custom-call | tf_op jit(solution)/shard_map/layer/pallas_call | solution.py:978
  233.0 8.7 %finish.1 = (bf16[2,64,3072]{2,1,0:T(8,128)(2,1)}, bf16[2,64,3072]{2,1,0:T(8,128)(2,1)}, f32[384,512]{1,0:T(8,128)}, f32[384,512]{1,0:T(8,128)}, f32[512,384]{1,0:T(8,128)}) custom-call(bf16[2,64,3072]{2,1,0:T(8,128)(2,1)} %x_ref.3, bf16[2,64,3072]{2,1,0:T(8,128)(2,1)} %dy_ref.3, f32[2,2,64,1536]{3,2,1,0:T(8,128)} %get-tuple-element.19.y_own, ...), custom_call_target="tpu_custom_call" | custom-call | tf_op jit(solution)/shard_map/finish/pallas_call | solution.py:924
